TPU v7x, 32 devices: a whole 2x2x4 slice. The times are simulated.
32 devices in a mesh: expert: 8 (over y, x, core), dp: 4 (over z).
Axes of the slice: x: 2, y: 2, z: 4, core: 2. Of those that a mesh axis runs over, the one named last changes fastest.
Arguments:
- out_grads: bfloat16 [4, 1024, 7168], P('dp', 'expert'), may hold values from -6 to 6
- expert_ids: int32 [4, 1024, 8], P('dp', 'expert'), may hold values from 0 to 63, all different within a row; in each aligned block of 128 rows (0 to 127, 128 to 255, ..., all dimensions but the last counted through in order) at most 24 rows name the same one
- gate_probs: float32 [4, 1024, 8], P('dp', 'expert'), may hold values from 0.05 to 0.5
- hidden_acts: bfloat16 [4, 64, 192, 2048], P('dp', 'expert'), may hold values from -6 to 6
- q_previous: bfloat16 [64, 32, 7168], P('expert'), may hold values from -0.0625 to 0.0625
Outputs:
- new_basis: float32 [64, 32, 2048], P('expert')
- q_update: float32 [64, 32, 7168], P('expert', None, 'dp')
Inputs may be any that keep to these rules, and one draw needn't show every extreme that they name: `expert_ids`: each row names 8 different experts; among the rows of one device no expert is named more than 24 times.
All inputs are finite; a program needn't handle non-finite values.
Results may differ from a plain program's by a relative error of at most 0.014.
Values may be sent and summed in bfloat16 or wider, within the bound.
A program may use at most 192 MiB of HBM per device.

v0:
```python
import functools
import math

import jax
import jax.numpy as jnp
from jax import lax
from jax.experimental import pallas as pl
from jax.experimental.pallas import tpu as pltpu
from jax.sharding import PartitionSpec as P

F32, BF16 = jnp.float32, jnp.bfloat16


MESH = pl.DeviceIdType.MESH


def orthonormal(value):
    rank = value[0].shape[0]
    rows = lax.broadcasted_iota(jnp.int32, (rank, 2 * rank), 0)
    cols = lax.broadcasted_iota(jnp.int32, (rank, 2 * rank), 1)
    eye = (cols == rows + rank).astype(F32)
    tables = []
    for one in value:
        doubled = jnp.concatenate([one, jnp.zeros_like(one)], axis=0)
        gram = lax.dot_general(
            one, doubled, (((1,), (1,)), ((), ())),
            precision=lax.Precision.HIGHEST, preferred_element_type=F32,
        )
        tables.append(gram + eye)
    for k in range(rank):
        for j, table in enumerate(tables):
            row = table[k : k + 1, :]
            pivot = lax.rsqrt(row[:, k : k + 1])
            scaled = row * pivot
            column = table[:, k : k + 1] * pivot
            table = jnp.where(rows > k, table - column * scaled, table)
            tables[j] = jnp.where(rows == k, scaled, table)
    return [
        jnp.dot(
            table[:, rank:], one, precision=lax.Precision.HIGHEST, preferred_element_type=F32
        )
        for table, one in zip(tables, value)
    ]


def factor_kernel(
    n, part_ref, hidden_ref, ortho_ref, proj_ref,
    hidden, got_part, fact, got_fact, load_sem, send_sem, recv_sem,
):
    me = lax.axis_index("dp")
    experts = hidden.shape[0]
    per = experts // n
    peers = [lax.rem(me + offset, n) for offset in range(1, n)]
    loads = []
    for j in range(experts):
        load = pltpu.make_async_copy(hidden_ref.at[j], hidden.at[j], load_sem.at[j])
        load.start()
        loads.append(load)
    barrier = pltpu.get_barrier_semaphore()
    for peer in peers:
        pl.semaphore_signal(barrier, inc=1, device_id={"dp": peer}, device_id_type=MESH)
    pl.semaphore_wait(barrier, n - 1)

    def push(phase, offset, source, target):
        copy = pltpu.make_async_remote_copy(
            src_ref=source,
            dst_ref=target,
            send_sem=send_sem.at[phase, offset],
            recv_sem=recv_sem.at[phase, offset],
            device_id={"dp": peers[offset]},
            device_id_type=MESH,
        )
        copy.start()
        return copy

    sent = [push(0, o, part_ref.at[peers[o]], got_part.at[o]) for o in range(n - 1)]
    for copy in sent:
        copy.wait()
    mixed = part_ref[me].astype(F32)
    for o in range(n - 1):
        mixed = mixed + got_part[o].astype(F32)
    mixed = mixed.astype(BF16)
    for load in loads:
        load.wait()
    rank = mixed.shape[1]
    for j in range(experts):
        fact[j] = jnp.dot(mixed[j], hidden[j], preferred_element_type=F32).astype(BF16)
    sent = [
        push(1, o, fact.at[pl.ds(peers[o] * per, per)], got_fact.at[o]) for o in range(n - 1)
    ]
    for copy in sent:
        copy.wait()
    share = []
    for i in range(per):
        total = fact[me * per + i].astype(F32)
        for o in range(n - 1):
            total = total + got_fact[o, i].astype(F32)
        share.append(total)
    for i, value in enumerate(orthonormal(share)):
        ortho_ref[me * per + i] = value.astype(BF16)
    mine = ortho_ref.at[pl.ds(me * per, per)]
    sent = [push(2, o, mine, mine) for o in range(n - 1)]

    def project(group):
        for i in range(per):
            j = group * per + i
            proj_ref[me, j] = lax.dot_general(
                ortho_ref[j], hidden[j], (((1,), (1,)), ((), ())), preferred_element_type=F32
            ).astype(BF16)

    project(me)
    for o in range(n - 1):
        sent[o].wait()
        project(lax.rem(me + n - 1 - o, n))
    sent = [push(3, o, proj_ref.at[me], proj_ref.at[me]) for o in range(n - 1)]
    for copy in sent:
        copy.wait()


def factors(part, hidden, n):
    experts, slots, units = hidden.shape
    rank = part.shape[2]
    per = experts // n
    vmem = pl.BlockSpec(memory_space=pltpu.VMEM)
    return pl.pallas_call(
        functools.partial(factor_kernel, n),
        out_shape=(
            jax.ShapeDtypeStruct((experts, rank, units), BF16),
            jax.ShapeDtypeStruct((n, experts, rank, slots), BF16),
        ),
        in_specs=[vmem, pl.BlockSpec(memory_space=pl.ANY)],
        out_specs=(vmem, vmem),
        scratch_shapes=[
            pltpu.VMEM((experts, slots, units), BF16),
            pltpu.VMEM((n - 1, experts, rank, slots), BF16),
            pltpu.VMEM((experts, rank, units), BF16),
            pltpu.VMEM((n - 1, per, rank, units), BF16),
            pltpu.SemaphoreType.DMA((experts,)),
            pltpu.SemaphoreType.DMA((4, n - 1)),
            pltpu.SemaphoreType.DMA((4, n - 1)),
        ],
        compiler_params=pltpu.CompilerParams(
            collective_id=0, has_side_effects=True, vmem_limit_bytes=40 * 2**20
        ),
        name="factors",
    )(part, hidden)


def gather_kernel(
    n_expert, n_dp, x_ref, all_ref,
    own_sem, z_send, z_recv, one_send, one_recv, two_send, two_recv, core_send, core_recv,
):
    me, z = lax.axis_index("expert"), lax.axis_index("dp")
    chips = n_expert // 2
    wide = math.isqrt(chips)
    sides = (wide, chips // wide)
    core, chip = lax.rem(me, 2), me // 2
    spot = (lax.rem(chip, wide), chip // wide)
    half, cols = x_ref.shape[0] // 2, all_ref.shape[3]

    def shifted(dim, by):
        return lax.rem(spot[dim] + by + sides[dim], sides[dim])

    def block(x, y, c):
        return (y * wide + x) * 2 + c

    def neighbour(dim, by):
        moved = shifted(dim, by)
        return block(moved, spot[1], core) if dim == 0 else block(spot[0], moved, core)

    def source(dim, first, second, c):
        x, y = (first, second) if dim == 0 else (second, first)
        return block(shifted(0, -x), shifted(1, -y), c)

    barrier = pltpu.get_barrier_semaphore()
    greeted = [{"dp": lax.rem(z + k, n_dp)} for k in range(1, n_dp)]
    greeted += [{"expert": neighbour(d, by)} for d in range(2) for by in range(1, sides[d])]
    greeted += [{"expert": block(spot[0], spot[1], 1 - core)}]
    for peer in greeted:
        pl.semaphore_signal(barrier, inc=1, device_id=peer, device_id_type=MESH)
    pl.semaphore_wait(barrier, len(greeted))

    sent = []

    def push(src, dst, send_sem, recv_sem, device):
        copy = pltpu.make_async_remote_copy(
            src_ref=src, dst_ref=dst, send_sem=send_sem, recv_sem=recv_sem,
            device_id=device, device_id_type=MESH,
        )
        copy.start()
        sent.append(copy)
        return copy

    def columns(r):
        return x_ref.at[:, pl.ds(pl.multiple_of(r * cols, 128), cols)]

    own = pltpu.make_async_copy(columns(z), all_ref.at[me, z], own_sem)
    own.start()
    arrive_z, arrive_one, arrive_two, arrive_core = {}, {}, {}, []
    for k in range(1, n_dp):
        to = lax.rem(z + k, n_dp)
        arrive_z[k] = push(
            columns(to), all_ref.at[me, z], z_send.at[k - 1], z_recv.at[k - 1], {"dp": to}
        )

    def rows(b, k, h):
        return all_ref.at[b, lax.rem(z - k + n_dp, n_dp), pl.ds(h * half, half)]

    def swap(k, h, first, second):
        part = rows(source(h, first, second, core), k, h)
        at = (h, k, first, second)
        partner = {"expert": block(spot[0], spot[1], 1 - core)}
        arrive_core.append(push(part, part, core_send.at[at], core_recv.at[at], partner))

    def onward(k, h, first):
        part = rows(source(h, first, 0, core), k, h)
        for by in range(1, sides[1 - h]):
            at = (h, k, first, by - 1)
            arrive_two[at] = push(
                part, part, two_send.at[at], two_recv.at[at], {"expert": neighbour(1 - h, by)}
            )
        swap(k, h, first, 0)

    for k in range(n_dp + 2):
        if k < n_dp:
            if k:
                arrive_z[k].wait_recv()
            else:
                own.wait()
            for h in range(2):
                part = rows(me, k, h)
                for by in range(1, sides[h]):
                    at = (h, k, by - 1)
                    arrive_one[at] = push(
                        part, part, one_send.at[at], one_recv.at[at], {"expert": neighbour(h, by)}
                    )
            for h in range(2):
                onward(k, h, 0)
        if 0 <= k - 1 < n_dp:
            for h in range(2):
                for by in range(1, sides[h]):
                    arrive_one[(h, k - 1, by - 1)].wait_recv()
                    onward(k - 1, h, by)
        if 0 <= k - 2 < n_dp:
            for h in range(2):
                for first in range(sides[h]):
                    for by in range(1, sides[1 - h]):
                        arrive_two[(h, k - 2, first, by - 1)].wait_recv()
                        swap(k - 2, h, first, by)
    for copy in arrive_core:
        copy.wait_recv()
    for copy in sent:
        copy.wait_send()


def gathered(grads):
    n_expert, n_dp = lax.axis_size("expert"), lax.axis_size("dp")
    tokens, width = grads.shape
    long = max(math.isqrt(n_expert // 2), n_expert // 2 // math.isqrt(n_expert // 2))
    dma = pltpu.SemaphoreType.DMA
    return pl.pallas_call(
        functools.partial(gather_kernel, n_expert, n_dp),
        out_shape=jax.ShapeDtypeStruct((n_expert, n_dp, tokens, width // n_dp), grads.dtype),
        in_specs=[pl.BlockSpec(memory_space=pltpu.VMEM)],
        out_specs=pl.BlockSpec(memory_space=pl.ANY),
        scratch_shapes=[
            dma(()), dma((n_dp - 1,)), dma((n_dp - 1,)),
            dma((2, n_dp, long)), dma((2, n_dp, long)),
            dma((2, n_dp, long, long)), dma((2, n_dp, long, long)),
            dma((2, n_dp, long, long)), dma((2, n_dp, long, long)),
        ],
        compiler_params=pltpu.CompilerParams(
            collective_id=1, has_side_effects=True, vmem_limit_bytes=56 * 2**20
        ),
        name="gather_rows",
    )(grads)


def local(out_grads, expert_ids, gate_probs, hidden_acts, q_previous):
    n_expert = lax.axis_size("expert")
    n_dp = lax.axis_size("dp")
    experts, slots, units = hidden_acts.shape[1:]
    capacity = slots // n_expert
    tokens, width = out_grads.shape[1:]
    top = expert_ids.shape[2]
    rank = q_previous.shape[1]
    cols = width // n_dp
    first = lax.axis_index("expert") * experts

    route = jnp.concatenate([expert_ids[0].astype(F32), gate_probs[0]], axis=1)
    route = lax.all_gather(route, ("dp", "expert"), axis=0)
    route = route.reshape(n_dp, n_expert, tokens, 2 * top)
    grads = gathered(out_grads[0])
    mine = (first + jnp.arange(experts)).astype(F32)[:, None]
    ids = route[..., :top].transpose(3, 0, 1, 2)[:, :, :, None, :]
    weight = route[..., top:].transpose(3, 0, 1, 2)[:, :, :, None, :]
    hit = ids == mine
    gate = jnp.sum(jnp.where(hit, weight, 0.0), axis=0)
    chosen = jnp.any(hit, axis=0)
    earlier = (jnp.arange(tokens)[:, None] < jnp.arange(tokens)[None, :]).astype(BF16)
    place = jnp.einsum("pbjt,tu->pbju", chosen.astype(BF16), earlier, preferred_element_type=F32)
    place = jnp.where(chosen, place, -1.0)
    pick = (place[:, :, :, None, :] == jnp.arange(capacity, dtype=F32)[:, None]).astype(BF16)

    q_part = lax.dynamic_slice_in_dim(q_previous, lax.axis_index("dp") * cols, cols, 2)
    mixed = jnp.einsum("jrd,bptd->jrbpt", q_part, grads, preferred_element_type=F32)
    scale = gate.transpose(2, 1, 0, 3)
    mixed = (mixed * scale[:, None]).astype(BF16)
    part = jnp.einsum("jrbpt,pbjct->pjrbc", mixed, pick, preferred_element_type=F32).astype(BF16)
    part = part.reshape(n_dp, experts, rank, slots)
    ortho, proj = factors(part, hidden_acts[0], n_dp)
    proj = proj.reshape(n_dp, experts, rank, n_expert, capacity)
    spread = jnp.einsum("pjrbc,pbjct->jrbpt", proj, pick, preferred_element_type=F32)
    spread = (spread * scale[:, None]).astype(BF16)
    q_update = jnp.einsum("jrbpt,bptd->jrd", spread, grads, preferred_element_type=F32)
    new_basis = ortho.astype(F32) * math.sqrt(units)
    return (new_basis, q_update)


def solution(mesh):
    return jax.shard_map(
        local,
        mesh=mesh,
        in_specs=(
            P("dp", "expert", None),
            P("dp", "expert", None),
            P("dp", "expert", None),
            P("dp", "expert", None, None),
            P("expert", None, None),
        ),
        out_specs=(P("expert", None, None), P("expert", None, "dp")),
        check_vma=False,
    )
```

profile of v0, /device:TPU:0, one launch (start us, length us, event | category | flops | bytes accessed | tf_op | source)
XLA Modules:
  0.0 235.0 jit_solution(11079083875436928144)
XLA Ops:
  0.6 0.7 convert_bitcast_fusion
  1.3 0.7 pad_maximum_fusion
  2.0 43.9 %all-gather = f32[4096,16]{0,1:T(8,128)S(1)} all-gather(f32[128,16]{0,1:T(8,128)S(1)} %pad_maximum_fusion), channel_id=2, replica_groups=mesh['expert'=8,'dp'=4] {'dp','expert'}, dimensions={0}, use_global_device_ids=true | all-gather | bytes 270336 | tf_op jit(solution)/shard_map/all_gather | solution.py:291
  45.9 0.1 copy.29
  46.0 0.2 fusion.18
  46.3 0.2 compare_reduce_fusion
  46.5 0.2 convolution_select_fusion
  46.6 0.1 copy.13
  46.7 71.5 %gather_rows.1 = bf16[8,4,128,1792]{3,2,1,0:T(8,128)(2,1)} custom-call(bf16[128,7168]{1,0:T(8,128)(2,1)} %bitcast.54), custom_call_target="tpu_custom_call" | custom-call | tf_op jit(solution)/shard_map/gather_rows/pallas_call | solution.py:261
  118.3 8.6 %fusion.7 = bf16[4,8,8,24,32]{4,3,2,1,0:T(8,128)(2,1)S(1)} fusion(f32[8,8,4,128]{3,1,0,2:T(8,128)S(1)} %copy.15, bf16[8,32,7168]{2,1,0:T(8,128)(2,1)} %param.9, s32[]{:T(128)S(6)} %select_n.12, bf16[8,4,128,1792]{3,2,1,0:T(8,128)(2,1)} %gather_rows.1, f32[4,8,8,128]{3,0,1,2:T(4,128)S(1)} %copy.13), kind=kOutput, calls=%fused_computation.12 | convolution fusion | flops 3811508224 | bytes 16252932 | tf_op jit(solution)/shard_map/jrbpt,pbjct->pjrbc/dot_general | solution.py:309
  126.9 0.8 copy.28.part_ref
  127.6 0.0 copy-start
  127.7 2.8 %copy-done = bf16[1,8,192,2048]{3,2,1,0:T(8,128)(2,1)S(1)} copy-done((bf16[1,8,192,2048]{3,2,1,0:T(8,128)(2,1)S(1)}, bf16[1,8,192,2048]{3,2,1,0:T(8,128)(2,1)}, u32[]{:S(2)}) %copy-start) | copy-done | bytes 6291480
  130.4 89.5 %factors.1 = (bf16[8,32,2048]{2,1,0:T(8,128)(2,1)S(1)}, bf16[4,8,32,192]{3,2,1,0:T(8,128)(2,1)S(1)}) custom-call(bf16[4,8,32,192]{3,2,1,0:T(8,128)(2,1)S(1)} %copy.28.part_ref, bf16[8,192,2048]{2,1,0:T(8,128)(2,1)S(1)} %bitcast.53), custom_call_target="tpu_custom_call" | custom-call | tf_op jit(solution)/shard_map/factors/pallas_call | solution.py:125
  220.0 2.6 %reshape.25 = bf16[4,8,32,8,24]{4,3,2,1,0:T(8,128)(2,1)} reshape(bf16[4,8,32,192]{3,2,1,0:T(8,128)(2,1)S(1)} %get-tuple-element.5) | data formatting | bytes 786432 | tf_op jit(solution)/shard_map/reshape | solution.py:312
  222.5 0.1 copy.19
  222.6 10.8 %convolution_bitcast_fusion = f32[8,32,1792]{2,1,0:T(8,128)} fusion(bf16[4,8,32,8,24]{4,3,2,1,0:T(8,128)(2,1)} %reshape.25, f32[8,8,4,128]{3,2,1,0:T(4,128)S(1)} %copy.19, bf16[8,4,128,1792]{3,2,1,0:T(8,128)(2,1)} %gather_rows.1, f32[4,8,8,128]{3,0,1,2:T(4,128)S(1)} %copy.13), kind=kOutput, calls=%fused_computation.7 | convolution fusion | flops 3811311616 | bytes 17170432 | tf_op jit(solution)/shard_map/jrbpt,bptd->jrd/dot_general | solution.py:315
  233.5 1.6 convert_multiply_fusion
  (3 shorter events, 0.1 us)
Async XLA Ops:
  127.6 2.8 %copy-start = (bf16[1,8,192,2048]{3,2,1,0:T(8,128)(2,1)S(1)}, bf16[1,8,192,2048]{3,2,1,0:T(8,128)(2,1)}, u32[]{:S(2)}) copy-start(bf16[1,8,192,2048]{3,2,1,0:T(8,128)(2,1)} %param.8) | copy-start | bytes 18874372
where the time goes:
time: 239 us; the launch traced here: 235 us
  Pallas kernels  161 us (67%)
  blocking collectives  43.9 us (18%)
  matrix products  19.6 us (8%)
  local copies, waits for them, and re-layouts  6.39 us (3%)
  other arithmetic  3.34 us (1%)
    pallas_call x1, Pallas kernels, factors(): pl.pallas_call(functools.partial(factor_kernel, n), out_shape=(jax.ShapeD...  89.5 us
    pallas_call x1, Pallas kernels, gathered(): pl.pallas_call(functools.partial(gather_kernel, n_expert, n_dp), out_shap...  71.5 us
    all_gather x1, blocking collectives, local(): route = lax.all_gather(route, ('dp', 'expert'), axis=0)  43.9 us
    dot_general x1, matrix products, local(): jnp.einsum('jrbpt,bptd->jrd', spread, grads, preferred_element_type=F32)  10.8 us
    dot_general x1, matrix products, local(): jnp.einsum('jrbpt,pbjct->pjrbc', mixed, pick, preferred_element_type=F32)  8.59 us

commit v1 on v0

--- a/solution.py
+++ b/solution.py
@@ -147,8 +147,8 @@
 
 
 def gather_kernel(
-    n_expert, n_dp, x_ref, all_ref,
-    own_sem, z_send, z_recv, one_send, one_recv, two_send, two_recv, core_send, core_recv,
+    n_expert, n_dp, x_ref, route_ref, all_ref, routes_ref,
+    route_send, route_recv, own_sem, z_send, z_recv, one_send, one_recv, two_send, two_recv, core_send, core_recv,
 ):
     me, z = lax.axis_index("expert"), lax.axis_index("dp")
     chips = n_expert // 2
@@ -173,14 +173,23 @@
         return block(shifted(0, -x), shifted(1, -y), c)
 
     barrier = pltpu.get_barrier_semaphore()
-    greeted = [{"dp": lax.rem(z + k, n_dp)} for k in range(1, n_dp)]
-    greeted += [{"expert": neighbour(d, by)} for d in range(2) for by in range(1, sides[d])]
-    greeted += [{"expert": block(spot[0], spot[1], 1 - core)}]
-    for peer in greeted:
-        pl.semaphore_signal(barrier, inc=1, device_id=peer, device_id_type=MESH)
-    pl.semaphore_wait(barrier, len(greeted))
+    def greet(i, carry):
+        pl.semaphore_signal(barrier, inc=1, device_id=other_of(i), device_id_type=MESH)
+        return carry
+
+    def other_of(i):
+        return {
+            "expert": lax.rem(me + lax.rem(i, n_expert), n_expert),
+            "dp": lax.rem(z + i // n_expert, n_dp),
+        }
+
+    total = n_expert * n_dp
+    lax.fori_loop(1, total, greet, 0)
+    pl.semaphore_wait(barrier, total - 1)
 
     sent = []
+    mine = routes_ref.at[z, me]
+    routes_ref[z, me] = route_ref[...]
 
     def push(src, dst, send_sem, recv_sem, device):
         copy = pltpu.make_async_remote_copy(
@@ -202,6 +211,15 @@
         arrive_z[k] = push(
             columns(to), all_ref.at[me, z], z_send.at[k - 1], z_recv.at[k - 1], {"dp": to}
         )
+
+    def tell(i, carry):
+        pltpu.make_async_remote_copy(
+            src_ref=route_ref, dst_ref=mine, send_sem=route_send.at[i],
+            recv_sem=route_recv.at[i], device_id=other_of(i), device_id_type=MESH,
+        ).start()
+        return carry
+
+    lax.fori_loop(1, total, tell, 0)
 
     def rows(b, k, h):
         return all_ref.at[b, lax.rem(z - k + n_dp, n_dp), pl.ds(h * half, half)]
@@ -247,24 +265,35 @@
                     for by in range(1, sides[1 - h]):
                         arrive_two[(h, k - 2, first, by - 1)].wait_recv()
                         swap(k - 2, h, first, by)
+    def told(i, carry):
+        pltpu.make_async_remote_copy(
+            src_ref=route_ref, dst_ref=mine, send_sem=route_send.at[i],
+            recv_sem=route_recv.at[i], device_id=other_of(i), device_id_type=MESH,
+        ).wait()
+        return carry
+
+    lax.fori_loop(1, total, told, 0)
     for copy in arrive_core:
         copy.wait_recv()
     for copy in sent:
         copy.wait_send()
 
 
-def gathered(grads):
+def gathered(grads, route):
     n_expert, n_dp = lax.axis_size("expert"), lax.axis_size("dp")
     tokens, width = grads.shape
     long = max(math.isqrt(n_expert // 2), n_expert // 2 // math.isqrt(n_expert // 2))
     dma = pltpu.SemaphoreType.DMA
     return pl.pallas_call(
         functools.partial(gather_kernel, n_expert, n_dp),
-        out_shape=jax.ShapeDtypeStruct((n_expert, n_dp, tokens, width // n_dp), grads.dtype),
-        in_specs=[pl.BlockSpec(memory_space=pltpu.VMEM)],
-        out_specs=pl.BlockSpec(memory_space=pl.ANY),
+        out_shape=(
+            jax.ShapeDtypeStruct((n_expert, n_dp, tokens, width // n_dp), grads.dtype),
+            jax.ShapeDtypeStruct((n_dp, n_expert, *route.shape), route.dtype),
+        ),
+        in_specs=[pl.BlockSpec(memory_space=pltpu.VMEM)] * 2,
+        out_specs=(pl.BlockSpec(memory_space=pl.ANY), pl.BlockSpec(memory_space=pltpu.VMEM)),
         scratch_shapes=[
-            dma(()), dma((n_dp - 1,)), dma((n_dp - 1,)),
+            dma((n_expert * n_dp,)), dma((n_expert * n_dp,)), dma(()), dma((n_dp - 1,)), dma((n_dp - 1,)),
             dma((2, n_dp, long)), dma((2, n_dp, long)),
             dma((2, n_dp, long, long)), dma((2, n_dp, long, long)),
             dma((2, n_dp, long, long)), dma((2, n_dp, long, long)),
@@ -273,7 +302,7 @@
             collective_id=1, has_side_effects=True, vmem_limit_bytes=56 * 2**20
         ),
         name="gather_rows",
-    )(grads)
+    )(grads, route)
 
 
 def local(out_grads, expert_ids, gate_probs, hidden_acts, q_previous):
@@ -287,13 +316,11 @@
     cols = width // n_dp
     first = lax.axis_index("expert") * experts
 
-    route = jnp.concatenate([expert_ids[0].astype(F32), gate_probs[0]], axis=1)
-    route = lax.all_gather(route, ("dp", "expert"), axis=0)
-    route = route.reshape(n_dp, n_expert, tokens, 2 * top)
-    grads = gathered(out_grads[0])
+    route = jnp.concatenate([expert_ids[0].astype(F32), gate_probs[0]], axis=1).T
+    grads, route = gathered(out_grads[0], route)
     mine = (first + jnp.arange(experts)).astype(F32)[:, None]
-    ids = route[..., :top].transpose(3, 0, 1, 2)[:, :, :, None, :]
-    weight = route[..., top:].transpose(3, 0, 1, 2)[:, :, :, None, :]
+    ids = route[:, :, :top].transpose(2, 0, 1, 3)[:, :, :, None, :]
+    weight = route[:, :, top:].transpose(2, 0, 1, 3)[:, :, :, None, :]
     hit = ids == mine
     gate = jnp.sum(jnp.where(hit, weight, 0.0), axis=0)
     chosen = jnp.any(hit, axis=0)

time: 239 us -> 207 us (0.87); the launches traced: 235 us -> 206 us
  blocking collectives: 43.9 us -> 0 us
  Pallas kernels: 161 us -> 174 us
    all_gather x1 -> x0, blocking collectives: 43.9 us -> none  [local(): route = lax.all_gather(route, ('dp', 'expert'), axis=0)]
    pallas_call x1, Pallas kernels: 71.5 us -> 82 us  [gathered(): pl.pallas_call(functools.partial(gather_kernel, n_expert, n_dp), out_shap...]
    pallas_call x1, Pallas kernels: 89.5 us -> 92.1 us  [factors(): pl.pallas_call(functools.partial(factor_kernel, n), out_shape=(jax.ShapeD...]
where the time goes in v1:
time: 207 us; the launch traced here: 206 us
  Pallas kernels  174 us (84%)
  matrix products  19.6 us (9%)
  local copies, waits for them, and re-layouts  7.36 us (4%)
  other arithmetic  3.94 us (2%)
    pallas_call x1, Pallas kernels, factors(): pl.pallas_call(functools.partial(factor_kernel, n), out_shape=(jax.ShapeD...  92.1 us
    pallas_call x1, Pallas kernels, gathered(): pl.pallas_call(functools.partial(gather_kernel, n_expert, n_dp), out_shap...  82 us
    dot_general x1, matrix products, local(): jnp.einsum('jrbpt,bptd->jrd', spread, grads, preferred_element_type=F32)  10.8 us
    dot_general x1, matrix products, local(): jnp.einsum('jrbpt,pbjct->pjrbc', mixed, pick, preferred_element_type=F32)  8.6 us

profile of v1, /device:TPU:0, one launch (start us, length us, event | category | flops | bytes accessed | tf_op | source)
XLA Modules:
  0.0 205.8 jit_solution(1566174713003165263)
XLA Ops:
  0.6 0.7 convert_bitcast_fusion
  1.3 1.3 maximum_bitcast_fusion.route_ref
  2.6 82.0 %gather_rows.1 = (bf16[8,4,128,1792]{3,2,1,0:T(8,128)(2,1)}, f32[4,8,16,128]{3,2,1,0:T(8,128)}) custom-call(bf16[128,7168]{1,0:T(8,128)(2,1)} %bitcast.51, f32[16,128]{1,0:T(8,128)} %maximum_bitcast_fusion.route_ref), custom_call_target="tpu_custom_call" | custom-call | tf_op jit(solution)/shard_map/gather_rows/pallas_call | solution.py:287
  84.7 1.0 slice_bitcast_fusion.1
  85.7 0.2 fusion.18
  86.0 0.2 compare_reduce_fusion
  86.2 0.2 convolution_select_fusion
  86.3 0.1 copy.18
  86.4 8.6 %fusion.7 = bf16[4,8,8,24,32]{4,3,2,1,0:T(8,128)(2,1)S(1)} fusion(f32[8,8,4,128]{3,1,0,2:T(8,128)S(1)} %copy.21, bf16[8,32,7168]{2,1,0:T(8,128)(2,1)} %param.9, s32[]{:T(128)S(6)} %select_n.12, bf16[8,4,128,1792]{3,2,1,0:T(8,128)(2,1)} %get-tuple-element.7, f32[4,8,8,128]{3,0,1,2:T(4,128)S(1)} %copy.18), kind=kOutput, calls=%fused_computation.12 | convolution fusion | flops 3811508224 | bytes 16252932 | tf_op jit(solution)/shard_map/jrbpt,pbjct->pjrbc/dot_general | solution.py:336
  95.0 0.8 copy.34.part_ref
  95.8 0.0 copy-start
  95.8 2.8 %copy-done = bf16[1,8,192,2048]{3,2,1,0:T(8,128)(2,1)S(1)} copy-done((bf16[1,8,192,2048]{3,2,1,0:T(8,128)(2,1)S(1)}, bf16[1,8,192,2048]{3,2,1,0:T(8,128)(2,1)}, u32[]{:S(2)}) %copy-start) | copy-done | bytes 6291480
  98.6 92.1 %factors.1 = (bf16[8,32,2048]{2,1,0:T(8,128)(2,1)S(1)}, bf16[4,8,32,192]{3,2,1,0:T(8,128)(2,1)S(1)}) custom-call(bf16[4,8,32,192]{3,2,1,0:T(8,128)(2,1)S(1)} %copy.34.part_ref, bf16[8,192,2048]{2,1,0:T(8,128)(2,1)S(1)} %bitcast.50), custom_call_target="tpu_custom_call" | custom-call | tf_op jit(solution)/shard_map/factors/pallas_call | solution.py:125
  190.7 2.6 %reshape.21 = bf16[4,8,32,8,24]{4,3,2,1,0:T(8,128)(2,1)} reshape(bf16[4,8,32,192]{3,2,1,0:T(8,128)(2,1)S(1)} %get-tuple-element.9) | data formatting | bytes 786432 | tf_op jit(solution)/shard_map/reshape | solution.py:339
  193.3 0.1 copy.25
  193.4 10.8 %convolution_bitcast_fusion = f32[8,32,1792]{2,1,0:T(8,128)} fusion(bf16[4,8,32,8,24]{4,3,2,1,0:T(8,128)(2,1)} %reshape.21, f32[8,8,4,128]{3,2,1,0:T(4,128)S(1)} %copy.25, bf16[8,4,128,1792]{3,2,1,0:T(8,128)(2,1)} %get-tuple-element.7, f32[4,8,8,128]{3,0,1,2:T(4,128)S(1)} %copy.18), kind=kOutput, calls=%fused_computation.7 | convolution fusion | flops 3811311616 | bytes 17170432 | tf_op jit(solution)/shard_map/jrbpt,bptd->jrd/dot_general | solution.py:342
  204.2 1.6 convert_multiply_fusion
  (4 shorter events, 0.1 us)
Async XLA Ops:
  95.8 2.8 %copy-start = (bf16[1,8,192,2048]{3,2,1,0:T(8,128)(2,1)S(1)}, bf16[1,8,192,2048]{3,2,1,0:T(8,128)(2,1)}, u32[]{:S(2)}) copy-start(bf16[1,8,192,2048]{3,2,1,0:T(8,128)(2,1)} %param.8) | copy-start | bytes 18874372

commit v2 on v1

--- a/solution.py
+++ b/solution.py
@@ -305,7 +305,434 @@
     )(grads, route)
 
 
+def fused_kernel(
+    n_expert, n_dp, grads_ref, route_ref, hidden_ref, q_ref, ortho_ref, upd_ref,
+    rep, bulk, hid, qv, routes, gate, pick, mixed, fact, got_up, got_cross, tot, gram, proj, spr,
+    load_sem, route_send, route_recv, far_send, far_recv, z_send, z_recv,
+    one_send, one_recv, two_send, two_recv, core_send, core_recv,
+    ring_send, ring_recv, proj_send, proj_recv,
+):
+    me, z = lax.axis_index("expert"), lax.axis_index("dp")
+    chips = n_expert // 2
+    wide = math.isqrt(chips)
+    sides = (wide, chips // wide)
+    core, chip = lax.rem(me, 2), me // 2
+    spot = (lax.rem(chip, wide), chip // wide)
+    tokens, cols = rep.shape[2:]
+    half = tokens // 2
+    experts, slots, units = hid.shape
+    rank = fact.shape[1]
+    cap = slots // n_expert
+    top = routes.shape[2] // 2
+    group = mixed.shape[0]
+    span = n_expert // group
+
+    def shifted(dim, by):
+        return lax.rem(spot[dim] + by + sides[dim], sides[dim])
+
+    def block(x, y, c):
+        return (y * wide + x) * 2 + c
+
+    def neighbour(dim, by):
+        moved = shifted(dim, by)
+        return block(moved, spot[1], core) if dim == 0 else block(spot[0], moved, core)
+
+    def source(dim, first, second, c):
+        x, y = (first, second) if dim == 0 else (second, first)
+        return block(shifted(0, -x), shifted(1, -y), c)
+
+    def beside(i):
+        return {"expert": lax.rem(me + i, n_expert)}
+
+    def along(k):
+        return {"dp": lax.rem(z + k, n_dp)}
+
+    loads = []
+
+    def load(src, dst):
+        copy = pltpu.make_async_copy(src, dst, load_sem.at[len(loads)])
+        copy.start()
+        loads.append(copy)
+
+    for k in range(n_dp):
+        load(grads_ref.at[:, pl.ds(k * cols, cols)], rep.at[k, me])
+    for k in range(n_dp):
+        load(q_ref.at[:, pl.ds(k * cols, cols)], qv.at[k])
+    for j in range(experts):
+        load(hidden_ref.at[j], hid.at[j])
+
+    barrier = pltpu.get_barrier_semaphore()
+    greeted = [along(k) for k in range(1, n_dp)] + [beside(i) for i in range(1, n_expert)]
+    for peer in greeted:
+        pl.semaphore_signal(barrier, inc=1, device_id=peer, device_id_type=MESH)
+    routes[0, me] = route_ref[...]
+    pl.semaphore_wait(barrier, len(greeted))
+
+    sent = []
+
+    def push(src, dst, send_sem, recv_sem, device):
+        copy = pltpu.make_async_remote_copy(
+            src_ref=src, dst_ref=dst, send_sem=send_sem, recv_sem=recv_sem,
+            device_id=device, device_id_type=MESH,
+        )
+        copy.start()
+        sent.append(copy)
+        return copy
+
+    told, told_far, arrive_z = {}, {}, {}
+    for i in range(1, n_expert):
+        told[0, i] = push(
+            route_ref, routes.at[0, me], route_send.at[0, i], route_recv.at[0, i], beside(i)
+        )
+    for k in range(1, n_dp):
+        told_far[k] = push(route_ref, routes.at[k, me], far_send.at[k], far_recv.at[k], along(k))
+
+    arrive_one, arrive_two, arrive_core = {}, {}, {}
+
+    def rows(b, k, h):
+        own = rep.at[k, b] if k < n_dp else bulk.at[k - n_dp, b]
+        return own.at[pl.ds(h * half, half)]
+
+    def swap(k, h, first, second):
+        part = rows(source(h, first, second, core), k, h)
+        at = (h, k, first, second)
+        partner = {"expert": block(spot[0], spot[1], 1 - core)}
+        arrive_core[at] = push(part, part, core_send.at[at], core_recv.at[at], partner)
+
+    def onward(k, h, first):
+        part = rows(source(h, first, 0, core), k, h)
+        for by in range(1, sides[1 - h]):
+            at = (h, k, first, by - 1)
+            arrive_two[at] = push(
+                part, part, two_send.at[at], two_recv.at[at], {"expert": neighbour(1 - h, by)}
+            )
+        swap(k, h, first, 0)
+
+    def begin(k):
+        for h in range(2):
+            part = rows(me, k, h)
+            for by in range(1, sides[h]):
+                at = (h, k, by - 1)
+                arrive_one[at] = push(
+                    part, part, one_send.at[at], one_recv.at[at], {"expert": neighbour(h, by)}
+                )
+        for h in range(2):
+            onward(k, h, 0)
+
+    def forward(k):
+        for h in range(2):
+            for by in range(1, sides[h]):
+                arrive_one[h, k, by - 1].wait_recv()
+                onward(k, h, by)
+
+    def second(k):
+        for h in range(2):
+            for first in range(sides[h]):
+                for by in range(1, sides[1 - h]):
+                    arrive_two[h, k, first, by - 1].wait_recv()
+                    swap(k, h, first, by)
+
+    def landed(k):
+        for at, copy in arrive_core.items():
+            if at[1] == k:
+                copy.wait_recv()
+
+    def accumulate(k):
+        for p in range(group):
+            piece = rep[k, p * span : (p + 1) * span].reshape(span * tokens, cols)
+            value = lax.dot_general(
+                qv[k], piece, (((1,), (1,)), ((), ())), preferred_element_type=F32
+            )
+            mixed[p] = value if k == 0 else mixed[p] + value
+
+    def place_tokens(k):
+        for i in range(1, n_expert):
+            told[k, i].wait_recv()
+        ours = lax.broadcasted_iota(jnp.int32, (experts, tokens), 0) + me * experts
+        ours = ours.astype(F32)
+        gates, hits = [], []
+        for b in range(n_expert):
+            table = routes[k, b]
+            value = jnp.zeros((experts, tokens), F32)
+            hit = jnp.zeros((experts, tokens), F32)
+            for t in range(top):
+                same = table[t : t + 1, :] == ours
+                value = jnp.where(same, table[top + t : top + t + 1, :], value)
+                hit = jnp.where(same, 1.0, hit)
+            gates.append(value)
+            hits.append(hit)
+        gate[k] = jnp.concatenate(gates, axis=1)
+        hits = jnp.concatenate(hits, axis=0)
+        before = lax.broadcasted_iota(jnp.int32, (tokens, tokens), 0)
+        after = lax.broadcasted_iota(jnp.int32, (tokens, tokens), 1)
+        earlier = jnp.where(before < after, 1.0, 0.0).astype(BF16)
+        count = jnp.dot(hits.astype(BF16), earlier, preferred_element_type=F32)
+        count = jnp.where(hits > 0.5, count, -float(slots))
+        keys = [
+            count[b * experts : (b + 1) * experts] + float(b * cap) for b in range(n_expert)
+        ]
+        key = jnp.concatenate(keys, axis=1).astype(jnp.int32)
+        level = lax.broadcasted_iota(jnp.int32, (slots, n_expert * tokens), 0)
+        for j in range(experts):
+            pick[k, j] = jnp.where(level == key[j : j + 1, :], 1.0, 0.0).astype(BF16)
+
+    for k in range(n_dp):
+        loads[k].wait()
+    for k in range(1, n_dp):
+        to = lax.rem(z + k, n_dp)
+        arrive_z[k] = push(
+            rep.at[to, me], bulk.at[k - 1, me], z_send.at[k], z_recv.at[k], along(k)
+        )
+    for k in range(n_dp + 3):
+        if k < n_dp:
+            begin(k)
+        if 0 <= k - 1 < n_dp:
+            forward(k - 1)
+        if k == 0:
+            place_tokens(0)
+        if k == n_dp:
+            for r in range(1, n_dp):
+                told_far[r].wait_recv()
+                for i in range(1, n_expert):
+                    told[r, i] = push(
+                        routes.at[r, me], routes.at[r, me],
+                        route_send.at[r, i], route_recv.at[r, i], beside(i),
+                    )
+            for r in range(1, n_dp):
+                arrive_z[r].wait_recv()
+                begin(n_dp + r - 1)
+        if 0 <= k - 2 < n_dp:
+            second(k - 2)
+        if 0 <= k - 3 < n_dp:
+            loads[n_dp + k - 3].wait()
+            landed(k - 3)
+            accumulate(k - 3)
+    for copy in loads[2 * n_dp :]:
+        copy.wait()
+
+    mate = z + 1 - 2 * lax.rem(z, 2)
+    cross = n_dp - 1 - z
+    inner = jnp.logical_or(z == 1, z == 2)
+
+    def hop(kind, j, src, dst, to):
+        return pltpu.make_async_remote_copy(
+            src_ref=src.at[j], dst_ref=dst.at[j],
+            send_sem=ring_send.at[kind, j], recv_sem=ring_recv.at[kind, j],
+            device_id={"dp": to}, device_id_type=MESH,
+        )
+
+    def up(j):
+        return hop(0, j, fact, got_up, mate)
+
+    def over(j):
+        return hop(1, j, fact, got_cross, cross)
+
+    def down(j):
+        return hop(2, j, tot, tot, mate)
+
+    for j in range(experts):
+        value = jnp.concatenate([mixed[p, j * rank : (j + 1) * rank] for p in range(group)], axis=1)
+        value = (value * gate[0, j : j + 1, :]).astype(BF16)
+        value = lax.dot_general(
+            value, pick[0, j], (((1,), (1,)), ((), ())), preferred_element_type=F32
+        ).astype(BF16)
+        fact[j] = jnp.dot(value, hid[j], preferred_element_type=F32).astype(BF16)
+
+        @pl.when(jnp.logical_not(inner))
+        def _():
+            up(j).start()
+
+    ahead = 2
+    others = list(range(1, n_dp))
+    for step in range(experts + ahead):
+        if step < experts:
+
+            @pl.when(inner)
+            def _():
+                up(step).wait_recv()
+                fact[step] = (fact[step].astype(F32) + got_up[step].astype(F32)).astype(BF16)
+                over(step).start()
+
+        if step >= ahead:
+            j = step - ahead
+
+            @pl.when(inner)
+            def _():
+                over(j).wait_recv()
+                tot[j] = (fact[j].astype(F32) + got_cross[j].astype(F32)).astype(BF16)
+                down(j).start()
+
+        if 1 <= step <= len(others):
+            place_tokens(others[step - 1])
+    for r in range(1, n_dp):
+        forward(n_dp + r - 1)
+
+    shape = (rank, 2 * rank)
+    eye = lax.broadcasted_iota(jnp.int32, shape, 1) == lax.broadcasted_iota(jnp.int32, shape, 0) + rank
+    eye = jnp.where(eye, 1.0, 0.0)
+    for j in range(experts):
+
+        @pl.when(jnp.logical_not(inner))
+        def _():
+            down(j).wait_recv()
+
+        one = tot[j]
+        doubled = jnp.concatenate([one, jnp.zeros_like(one)], axis=0)
+        gram[j] = eye + lax.dot_general(
+            one, doubled, (((1,), (1,)), ((), ())), preferred_element_type=F32
+        )
+
+    table = [gram[:, k, :] for k in range(rank)]
+    for k in range(rank):
+        row = table[k]
+        scaled = row / row[:, k : k + 1]
+        for i in range(k + 1, rank):
+            table[i] = table[i] - row[:, i : i + 1] * scaled
+        table[k] = row * lax.rsqrt(row[:, k : k + 1])
+    for k in range(rank):
+        gram[:, k, :] = table[k]
+
+    batch = experts // 2
+    arrive_proj = {}
+    for j in range(experts):
+        inverse = gram[j][:, rank:]
+        high = inverse.astype(BF16)
+        low = (inverse - high.astype(F32)).astype(BF16)
+        one = tot[j]
+        value = jnp.dot(high, one, preferred_element_type=F32)
+        value = (value + jnp.dot(low, one, preferred_element_type=F32)).astype(BF16)
+        ortho_ref[j] = value
+        proj[0, j // 2, :, (j % 2) * slots : (j % 2 + 1) * slots] = lax.dot_general(
+            value, hid[j], (((1,), (1,)), ((), ())), preferred_element_type=F32
+        ).astype(BF16)
+        if (j + 1) % batch == 0:
+            g = j // batch
+            part = pl.ds(g * batch // 2, batch // 2)
+            for k in range(1, n_dp):
+                arrive_proj[k, g] = push(
+                    proj.at[0, part], proj.at[k, part],
+                    proj_send.at[k, g], proj_recv.at[k, g], along(k),
+                )
+
+    def update(k):
+        if k:
+            for g in range(2):
+                arrive_proj[k, g].wait_recv()
+        for j in range(experts):
+            value = jnp.dot(
+                proj[k, j // 2, :, (j % 2) * slots : (j % 2 + 1) * slots], pick[k, j],
+                preferred_element_type=F32,
+            )
+            spr[j * rank : (j + 1) * rank] = (value * gate[k, j : j + 1, :]).astype(BF16)
+        if k:
+            landed(n_dp + k - 1)
+        own = bulk.at[k - 1] if k else rep.at[z]
+
+        def tile(c, carry):
+            at = pl.ds(pl.multiple_of(c * 256, 256), 256)
+            right = own[:, :, at].reshape(n_expert * tokens, 256)
+            value = jnp.dot(spr[...], right, preferred_element_type=F32)
+            upd_ref[:, at] = upd_ref[:, at] + value if k else value
+            return carry
+
+        lax.fori_loop(0, cols // 256, tile, 0)
+
+    update(0)
+    for r in range(1, n_dp):
+        second(n_dp + r - 1)
+    for r in range(1, n_dp):
+        update(r)
+    for j in range(experts):
+
+        @pl.when(inner)
+        def _():
+            over(j).wait_send()
+            down(j).wait_send()
+
+        @pl.when(jnp.logical_not(inner))
+        def _():
+            up(j).wait_send()
+
+    for copy in sent:
+        copy.wait_send()
+
+
+def fused_buffers(n_expert, n_dp, tokens, width, experts, slots, units, rank, top):
+    cols = width // n_dp
+    return [
+        ((n_dp, n_expert, tokens, cols), BF16),
+        ((n_dp - 1, n_expert, tokens, cols), BF16),
+        ((experts, slots, units), BF16),
+        ((n_dp, experts * rank, cols), BF16),
+        ((n_dp, n_expert, 2 * top, tokens), F32),
+        ((n_dp, experts, n_expert * tokens), F32),
+        ((n_dp, experts, slots, n_expert * tokens), BF16),
+        ((n_expert // 2, experts * rank, 2 * tokens), F32),
+        ((experts, rank, units), BF16),
+        ((experts, rank, units), BF16),
+        ((experts, rank, units), BF16),
+        ((experts, rank, units), BF16),
+        ((experts, rank, 2 * rank), F32),
+        ((n_dp, experts // 2, rank, 2 * slots), BF16),
+        ((experts * rank, n_expert * tokens), BF16),
+    ]
+
+
+def fused(grads, route, hidden, q, buffers):
+    n_expert, n_dp = lax.axis_size("expert"), lax.axis_size("dp")
+    experts, slots, units = hidden.shape
+    rank = q.shape[0] // experts
+    cols = q.shape[1] // n_dp
+    chips = n_expert // 2
+    long = max(math.isqrt(chips), chips // math.isqrt(chips))
+    tags = 2 * n_dp - 1
+    dma = pltpu.SemaphoreType.DMA
+    vmem = pl.BlockSpec(memory_space=pltpu.VMEM)
+    anywhere = pl.BlockSpec(memory_space=pl.ANY)
+    return pl.pallas_call(
+        functools.partial(fused_kernel, n_expert, n_dp),
+        out_shape=(
+            jax.ShapeDtypeStruct((experts, rank, units), BF16),
+            jax.ShapeDtypeStruct((experts * rank, cols), F32),
+        ),
+        in_specs=[anywhere, vmem, anywhere, anywhere],
+        out_specs=(vmem, vmem),
+        scratch_shapes=[pltpu.VMEM(*b) for b in buffers] + [
+            dma((2 * n_dp + experts,)),
+            dma((n_dp, n_expert)), dma((n_dp, n_expert)), dma((n_dp,)), dma((n_dp,)),
+            dma((n_dp,)), dma((n_dp,)),
+            dma((2, tags, long)), dma((2, tags, long)),
+            dma((2, tags, long, long)), dma((2, tags, long, long)),
+            dma((2, tags, long, long)), dma((2, tags, long, long)),
+            dma((3, experts)), dma((3, experts)), dma((n_dp, 2)), dma((n_dp, 2)),
+        ],
+        compiler_params=pltpu.CompilerParams(
+            collective_id=2, has_side_effects=True, vmem_limit_bytes=67043328
+        ),
+        name="fused",
+    )(grads, route, hidden, q)
+
+
 def local(out_grads, expert_ids, gate_probs, hidden_acts, q_previous):
+    n_expert, n_dp = lax.axis_size("expert"), lax.axis_size("dp")
+    experts, slots, units = hidden_acts.shape[1:]
+    tokens, width = out_grads.shape[1:]
+    rank = q_previous.shape[1]
+    cols = width // n_dp
+    buffers = fused_buffers(
+        n_expert, n_dp, tokens, width, experts, slots, units, rank, expert_ids.shape[2]
+    )
+    held = sum(math.prod(shape) * jnp.dtype(kind).itemsize for shape, kind in buffers)
+    held += experts * rank * (4 * cols + 2 * units)
+    if n_dp != 4 or held > 60 * 2**20:
+        return spacious(out_grads, expert_ids, gate_probs, hidden_acts, q_previous)
+    route = jnp.concatenate([expert_ids[0].astype(F32), gate_probs[0]], axis=1).T
+    q = q_previous.reshape(experts * rank, width)
+    ortho, update = fused(out_grads[0], route, hidden_acts[0], q, buffers)
+    return (ortho.astype(F32) * math.sqrt(units), update.reshape(experts, rank, cols))
+
+
+def spacious(out_grads, expert_ids, gate_probs, hidden_acts, q_previous):
     n_expert = lax.axis_size("expert")
     n_dp = lax.axis_size("dp")
     experts, slots, units = hidden_acts.shape[1:]

time: 207 us -> 146 us (0.71)
  Pallas kernels: 174 us -> 139 us
  matrix products: 19.6 us -> 0 us
  local copies, waits for them, and re-layouts: 7.36 us -> 1.23 us
    pallas_call x2 -> x1, Pallas kernels: 174 us -> 139 us  [fused(): pl.pallas_call(functools.partial(fused_kernel, n_expert, n_dp), out_shape...]
    dot_general x3 -> x0, matrix products: 19.6 us -> none  [the longest x1 10.8 us: local(): jnp.einsum('jrbpt,bptd->jrd', spread, grads, preferred_element_type=F32)]
    reshape x2 -> x0, local copies, waits for them, and re-layouts: 3.34 us -> none  [the longest x1 2.58 us: local(): proj = proj.reshape(n_dp, experts, rank, n_expert, capacity)]
where the time goes in v2:
time: 146 us
  Pallas kernels  139 us (95%)
  other arithmetic  4.91 us (3%)
    pallas_call x1, Pallas kernels, fused(): pl.pallas_call(functools.partial(fused_kernel, n_expert, n_dp), out_shape...  139 us
    mul x1, other arithmetic, local(): ortho.astype(F32) * math.sqrt(units)  2.93 us

profile of v2, /device:TPU:0, one launch (start us, length us, event | category | flops | bytes accessed | tf_op | source)
XLA Modules:
  0.0 145.9 jit_solution(15215045355381672349)
XLA Ops:
  0.6 0.7 convert_bitcast_fusion
  1.3 1.3 maximum_bitcast_fusion.route_ref
  2.6 139.1 %fused.1 = (bf16[8,32,2048]{2,1,0:T(8,128)(2,1)}, f32[256,1792]{1,0:T(8,128)}) custom-call(bf16[128,7168]{1,0:T(8,128)(2,1)} %bitcast.11, f32[16,128]{1,0:T(8,128)} %maximum_bitcast_fusion.route_ref, bf16[8,192,2048]{2,1,0:T(8,128)(2,1)} %bitcast.9, bf16[256,7168]{1,0:T(8,128)(2,1)} %bitcast.10), custom_call_target="tpu_custom_call" | custom-call | tf_op jit(solution)/shard_map/fused/pallas_call | solution.py:692
  141.8 0.0 copy-start
  141.8 2.9 %convert_multiply_fusion = f32[8,32,2048]{2,1,0:T(8,128)} fusion(bf16[8,32,2048]{2,1,0:T(8,128)(2,1)} %get-tuple-element.4), kind=kLoop, calls=%fused_computation | loop fusion | flops 1048576 | bytes 3145728 | tf_op jit(solution)/shard_map/mul | solution.py:732
  144.7 0.0 copy-done
  144.7 1.2 copy.8
Async XLA Ops:
  141.8 2.9 %copy-start = (f32[256,1792]{1,0:T(8,128)S(1)}, f32[256,1792]{1,0:T(8,128)}, u32[]{:S(2)}) copy-start(f32[256,1792]{1,0:T(8,128)} %get-tuple-element.5) | copy-start | bytes 5505028

commit v3 on v2

--- a/solution.py
+++ b/solution.py
@@ -306,9 +306,9 @@
 
 
 def fused_kernel(
-    n_expert, n_dp, grads_ref, route_ref, hidden_ref, q_ref, ortho_ref, upd_ref,
+    n_expert, n_dp, grads_ref, ids_ref, probs_ref, hidden_ref, q_ref, basis_ref, upd_ref,
     rep, bulk, hid, qv, routes, gate, pick, mixed, fact, got_up, got_cross, tot, gram, proj, spr,
-    load_sem, route_send, route_recv, far_send, far_recv, z_send, z_recv,
+    basis, upd, out_sem, load_sem, route_send, route_recv, far_send, far_recv, z_send, z_recv,
     one_send, one_recv, two_send, two_recv, core_send, core_recv,
     ring_send, ring_recv, proj_send, proj_recv,
 ):
@@ -321,7 +321,7 @@
     tokens, cols = rep.shape[2:]
     half = tokens // 2
     experts, slots, units = hid.shape
-    rank = fact.shape[1]
+    rank = 2 * fact.shape[1]
     cap = slots // n_expert
     top = routes.shape[2] // 2
     group = mixed.shape[0]
@@ -365,7 +365,8 @@
     greeted = [along(k) for k in range(1, n_dp)] + [beside(i) for i in range(1, n_expert)]
     for peer in greeted:
         pl.semaphore_signal(barrier, inc=1, device_id=peer, device_id_type=MESH)
-    routes[0, me] = route_ref[...]
+    routes[0, me] = jnp.concatenate([ids_ref[...].astype(F32), probs_ref[...]], axis=0)
+    own_route = routes.at[0, me]
     pl.semaphore_wait(barrier, len(greeted))
 
     sent = []
@@ -382,10 +383,10 @@
     told, told_far, arrive_z = {}, {}, {}
     for i in range(1, n_expert):
         told[0, i] = push(
-            route_ref, routes.at[0, me], route_send.at[0, i], route_recv.at[0, i], beside(i)
+            own_route, own_route, route_send.at[0, i], route_recv.at[0, i], beside(i)
         )
     for k in range(1, n_dp):
-        told_far[k] = push(route_ref, routes.at[k, me], far_send.at[k], far_recv.at[k], along(k))
+        told_far[k] = push(own_route, routes.at[k, me], far_send.at[k], far_recv.at[k], along(k))
 
     arrive_one, arrive_two, arrive_core = {}, {}, {}
 
@@ -425,9 +426,9 @@
                 arrive_one[h, k, by - 1].wait_recv()
                 onward(k, h, by)
 
-    def second(k):
+    def second(k, low=0, high=None):
         for h in range(2):
-            for first in range(sides[h]):
+            for first in range(low, sides[h] if high is None else high):
                 for by in range(1, sides[1 - h]):
                     arrive_two[h, k, first, by - 1].wait_recv()
                     swap(k, h, first, by)
@@ -437,13 +438,26 @@
             if at[1] == k:
                 copy.wait_recv()
 
+    def gain(k, p):
+        piece = rep[k, pl.ds(p * span, span)].reshape(span * tokens, cols)
+        value = lax.dot_general(
+            qv[k], piece, (((1,), (1,)), ((), ())), preferred_element_type=F32
+        )
+        mixed[p] = value if k == 0 else mixed[p] + value
+
     def accumulate(k):
+        loads[n_dp + k].wait()
+        landed(k)
         for p in range(group):
-            piece = rep[k, p * span : (p + 1) * span].reshape(span * tokens, cols)
-            value = lax.dot_general(
-                qv[k], piece, (((1,), (1,)), ((), ())), preferred_element_type=F32
-            )
-            mixed[p] = value if k == 0 else mixed[p] + value
+            gain(k, p)
+
+    def finish(k, far):
+        for x in range(sides[0]):
+            for y in range(sides[1]):
+                if (x > 0 and y > 0) == far:
+                    arrive_core[0, k, x, y].wait_recv()
+                    arrive_core[1, k, y, x].wait_recv()
+                    gain(k, source(0, x, y, 0) // 2)
 
     def place_tokens(k):
         for i in range(1, n_expert):
@@ -483,7 +497,7 @@
         arrive_z[k] = push(
             rep.at[to, me], bulk.at[k - 1, me], z_send.at[k], z_recv.at[k], along(k)
         )
-    for k in range(n_dp + 3):
+    for k in range(n_dp + 2):
         if k < n_dp:
             begin(k)
         if 0 <= k - 1 < n_dp:
@@ -501,12 +515,16 @@
             for r in range(1, n_dp):
                 arrive_z[r].wait_recv()
                 begin(n_dp + r - 1)
-        if 0 <= k - 2 < n_dp:
+        if 0 <= k - 3 < n_dp - 1:
+            accumulate(k - 3)
+        if 0 <= k - 2 < n_dp - 1:
             second(k - 2)
-        if 0 <= k - 3 < n_dp:
-            loads[n_dp + k - 3].wait()
-            landed(k - 3)
-            accumulate(k - 3)
+        if k == n_dp + 1:
+            second(n_dp - 1, 0, 1)
+    loads[2 * n_dp - 1].wait()
+    finish(n_dp - 1, False)
+    second(n_dp - 1, 1)
+    finish(n_dp - 1, True)
     for copy in loads[2 * n_dp :]:
         copy.wait()
 
@@ -536,16 +554,19 @@
         value = lax.dot_general(
             value, pick[0, j], (((1,), (1,)), ((), ())), preferred_element_type=F32
         ).astype(BF16)
-        fact[j] = jnp.dot(value, hid[j], preferred_element_type=F32).astype(BF16)
+        value = jnp.dot(value, hid[j], preferred_element_type=F32).astype(BF16)
+        fact[2 * j : 2 * j + 2] = value.reshape(2, rank // 2, units)
 
         @pl.when(jnp.logical_not(inner))
         def _():
-            up(j).start()
-
-    ahead = 2
+            up(2 * j).start()
+            up(2 * j + 1).start()
+
+    ahead = 3
+    pieces = 2 * experts
     others = list(range(1, n_dp))
-    for step in range(experts + ahead):
-        if step < experts:
+    for step in range(pieces + ahead):
+        if step < pieces:
 
             @pl.when(inner)
             def _():
@@ -562,8 +583,8 @@
                 tot[j] = (fact[j].astype(F32) + got_cross[j].astype(F32)).astype(BF16)
                 down(j).start()
 
-        if 1 <= step <= len(others):
-            place_tokens(others[step - 1])
+        if step % 2 == 1 and step // 2 < len(others):
+            place_tokens(others[step // 2])
     for r in range(1, n_dp):
         forward(n_dp + r - 1)
 
@@ -574,39 +595,48 @@
 
         @pl.when(jnp.logical_not(inner))
         def _():
-            down(j).wait_recv()
-
-        one = tot[j]
+            down(2 * j).wait_recv()
+            down(2 * j + 1).wait_recv()
+
+        one = tot[2 * j : 2 * j + 2].reshape(rank, units)
         doubled = jnp.concatenate([one, jnp.zeros_like(one)], axis=0)
         gram[j] = eye + lax.dot_general(
             one, doubled, (((1,), (1,)), ((), ())), preferred_element_type=F32
         )
 
-    table = [gram[:, k, :] for k in range(rank)]
+    table = [gram[:, k, :].T for k in range(rank)]
     for k in range(rank):
         row = table[k]
-        scaled = row / row[:, k : k + 1]
+        scaled = row * (1.0 / row[k : k + 1, :])
         for i in range(k + 1, rank):
-            table[i] = table[i] - row[:, i : i + 1] * scaled
-        table[k] = row * lax.rsqrt(row[:, k : k + 1])
+            table[i] = table[i] - row[i : i + 1, :] * scaled
+        table[k] = row * lax.rsqrt(row[k : k + 1, :])
     for k in range(rank):
-        gram[:, k, :] = table[k]
+        gram[:, k, :] = table[k].T
 
     batch = experts // 2
-    arrive_proj = {}
+    arrive_proj, stored = {}, []
+
+    def put(src, dst):
+        copy = pltpu.make_async_copy(src, dst, out_sem.at[len(stored)])
+        copy.start()
+        stored.append(copy)
+
     for j in range(experts):
         inverse = gram[j][:, rank:]
         high = inverse.astype(BF16)
         low = (inverse - high.astype(F32)).astype(BF16)
-        one = tot[j]
+        one = tot[2 * j : 2 * j + 2].reshape(rank, units)
         value = jnp.dot(high, one, preferred_element_type=F32)
-        value = (value + jnp.dot(low, one, preferred_element_type=F32)).astype(BF16)
-        ortho_ref[j] = value
+        value = value + jnp.dot(low, one, preferred_element_type=F32)
+        basis[j] = value * math.sqrt(units)
+        value = value.astype(BF16)
         proj[0, j // 2, :, (j % 2) * slots : (j % 2 + 1) * slots] = lax.dot_general(
             value, hid[j], (((1,), (1,)), ((), ())), preferred_element_type=F32
         ).astype(BF16)
         if (j + 1) % batch == 0:
             g = j // batch
+            put(basis.at[pl.ds(g * batch, batch)], basis_ref.at[pl.ds(g * batch, batch)])
             part = pl.ds(g * batch // 2, batch // 2)
             for k in range(1, n_dp):
                 arrive_proj[k, g] = push(
@@ -628,21 +658,21 @@
             landed(n_dp + k - 1)
         own = bulk.at[k - 1] if k else rep.at[z]
 
-        def tile(c, carry):
-            at = pl.ds(pl.multiple_of(c * 256, 256), 256)
-            right = own[:, :, at].reshape(n_expert * tokens, 256)
+        width = 256 if cols % 256 == 0 else 128
+        for c in range(cols // width):
+            at = slice(c * width, (c + 1) * width)
+            right = own[:, :, at].reshape(n_expert * tokens, width)
             value = jnp.dot(spr[...], right, preferred_element_type=F32)
-            upd_ref[:, at] = upd_ref[:, at] + value if k else value
-            return carry
-
-        lax.fori_loop(0, cols // 256, tile, 0)
+            upd[:, at] = upd[:, at] + value if k else value
+            if k == n_dp - 1:
+                put(upd.at[:, at], upd_ref.at[:, at])
 
     update(0)
     for r in range(1, n_dp):
         second(n_dp + r - 1)
     for r in range(1, n_dp):
         update(r)
-    for j in range(experts):
+    for j in range(pieces):
 
         @pl.when(inner)
         def _():
@@ -655,6 +685,8 @@
 
     for copy in sent:
         copy.wait_send()
+    for copy in stored:
+        copy.wait()
 
 
 def fused_buffers(n_expert, n_dp, tokens, width, experts, slots, units, rank, top):
@@ -668,17 +700,19 @@
         ((n_dp, experts, n_expert * tokens), F32),
         ((n_dp, experts, slots, n_expert * tokens), BF16),
         ((n_expert // 2, experts * rank, 2 * tokens), F32),
-        ((experts, rank, units), BF16),
-        ((experts, rank, units), BF16),
-        ((experts, rank, units), BF16),
-        ((experts, rank, units), BF16),
+        ((2 * experts, rank // 2, units), BF16),
+        ((2 * experts, rank // 2, units), BF16),
+        ((2 * experts, rank // 2, units), BF16),
+        ((2 * experts, rank // 2, units), BF16),
         ((experts, rank, 2 * rank), F32),
         ((n_dp, experts // 2, rank, 2 * slots), BF16),
         ((experts * rank, n_expert * tokens), BF16),
+        ((experts, rank, units), F32),
+        ((experts * rank, cols), F32),
     ]
 
 
-def fused(grads, route, hidden, q, buffers):
+def fused(grads, ids, probs, hidden, q, buffers):
     n_expert, n_dp = lax.axis_size("expert"), lax.axis_size("dp")
     experts, slots, units = hidden.shape
     rank = q.shape[0] // experts
@@ -692,25 +726,25 @@
     return pl.pallas_call(
         functools.partial(fused_kernel, n_expert, n_dp),
         out_shape=(
-            jax.ShapeDtypeStruct((experts, rank, units), BF16),
+            jax.ShapeDtypeStruct((experts, rank, units), F32),
             jax.ShapeDtypeStruct((experts * rank, cols), F32),
         ),
-        in_specs=[anywhere, vmem, anywhere, anywhere],
-        out_specs=(vmem, vmem),
+        in_specs=[anywhere, vmem, vmem, anywhere, anywhere],
+        out_specs=(anywhere, anywhere),
         scratch_shapes=[pltpu.VMEM(*b) for b in buffers] + [
-            dma((2 * n_dp + experts,)),
+            dma((2 + cols // 128,)), dma((2 * n_dp + experts,)),
             dma((n_dp, n_expert)), dma((n_dp, n_expert)), dma((n_dp,)), dma((n_dp,)),
             dma((n_dp,)), dma((n_dp,)),
-            dma((2, tags, long)), dma((2, tags, long)),
+            dma((2, tags, long - 1)), dma((2, tags, long - 1)),
+            dma((2, tags, long, long - 1)), dma((2, tags, long, long - 1)),
             dma((2, tags, long, long)), dma((2, tags, long, long)),
-            dma((2, tags, long, long)), dma((2, tags, long, long)),
-            dma((3, experts)), dma((3, experts)), dma((n_dp, 2)), dma((n_dp, 2)),
+            dma((3, 2 * experts)), dma((3, 2 * experts)), dma((n_dp, 2)), dma((n_dp, 2)),
         ],
         compiler_params=pltpu.CompilerParams(
             collective_id=2, has_side_effects=True, vmem_limit_bytes=67043328
         ),
         name="fused",
-    )(grads, route, hidden, q)
+    )(grads, ids, probs, hidden, q)
 
 
 def local(out_grads, expert_ids, gate_probs, hidden_acts, q_previous):
@@ -723,13 +757,11 @@
         n_expert, n_dp, tokens, width, experts, slots, units, rank, expert_ids.shape[2]
     )
     held = sum(math.prod(shape) * jnp.dtype(kind).itemsize for shape, kind in buffers)
-    held += experts * rank * (4 * cols + 2 * units)
     if n_dp != 4 or held > 60 * 2**20:
         return spacious(out_grads, expert_ids, gate_probs, hidden_acts, q_previous)
-    route = jnp.concatenate([expert_ids[0].astype(F32), gate_probs[0]], axis=1).T
     q = q_previous.reshape(experts * rank, width)
-    ortho, update = fused(out_grads[0], route, hidden_acts[0], q, buffers)
-    return (ortho.astype(F32) * math.sqrt(units), update.reshape(experts, rank, cols))
+    basis, update = fused(out_grads[0], expert_ids[0].T, gate_probs[0].T, hidden_acts[0], q, buffers)
+    return (basis, update.reshape(experts, rank, cols))
 
 
 def spacious(out_grads, expert_ids, gate_probs, hidden_acts, q_previous):

time: 146 us -> 131 us (0.90)
  Pallas kernels: 139 us -> 125 us
  other arithmetic: 4.91 us -> 0 us
  local copies, waits for them, and re-layouts: 1.23 us -> 4.5 us
    pallas_call x1, Pallas kernels: 139 us -> 125 us  [fused(): pl.pallas_call(functools.partial(fused_kernel, n_expert, n_dp), out_shape...]
    unnamed x3 -> x4, local copies, waits for them, and re-layouts: 1.23 us -> 4.5 us
    mul x1 -> x0, other arithmetic: 2.93 us -> none  [local(): ortho.astype(F32) * math.sqrt(units)]
where the time goes in v3:
time: 131 us; the launch traced here: 130 us
  Pallas kernels  125 us (95%)
  local copies, waits for them, and re-layouts  4.5 us (3%)
    pallas_call x1, Pallas kernels, fused(): pl.pallas_call(functools.partial(fused_kernel, n_expert, n_dp), out_shape...  125 us
    unnamed x4, local copies, waits for them, and re-layouts  4.5 us

profile of v3, /device:TPU:0, one launch (start us, length us, event | category | flops | bytes accessed | tf_op | source)
XLA Modules:
  0.0 130.3 jit_solution(10457386449022131595)
XLA Ops:
  0.6 125.1 %fused.1 = (f32[8,32,2048]{2,1,0:T(8,128)}, f32[256,1792]{1,0:T(8,128)}) custom-call(bf16[128,7168]{1,0:T(8,128)(2,1)} %bitcast.12, s32[8,128]{1,0:T(8,128)} %bitcast.14, f32[8,128]{1,0:T(8,128)} %bitcast.15, bf16[8,192,2048]{2,1,0:T(8,128)(2,1)} %bitcast.10, bf16[256,7168]{1,0:T(8,128)(2,1)} %bitcast.11), custom_call_target="tpu_custom_call" | custom-call | tf_op jit(solution)/shard_map/fused/pallas_call | solution.py:726
  125.8 0.0 copy-start
  125.8 3.3 %copy.9 = f32[8,32,2048]{2,1,0:T(8,128)} copy(f32[8,32,2048]{2,1,0:T(8,128)} %get-tuple-element.8) | data formatting | bytes 4194304
  129.1 0.0 copy-done
  129.1 1.2 copy.10
Async XLA Ops:
  125.8 3.3 %copy-start = (f32[256,1792]{1,0:T(8,128)S(1)}, f32[256,1792]{1,0:T(8,128)}, u32[]{:S(2)}) copy-start(f32[256,1792]{1,0:T(8,128)} %get-tuple-element.5) | copy-start | bytes 5505028

commit v4 on v3

--- a/solution.py
+++ b/solution.py
@@ -307,9 +307,10 @@
 
 def fused_kernel(
     n_expert, n_dp, grads_ref, ids_ref, probs_ref, hidden_ref, q_ref, basis_ref, upd_ref,
-    rep, bulk, hid, qv, routes, gate, pick, mixed, fact, got_up, got_cross, tot, gram, proj, spr,
-    basis, upd, out_sem, load_sem, route_send, route_recv, far_send, far_recv, z_send, z_recv,
-    one_send, one_recv, two_send, two_recv, core_send, core_recv,
+    rep, own, hid, qall, routes, gate, pick, near_gate, near_pick, weighed, message, parts, spots,
+    fact, got_up, got_cross, tot, gram, proj, spr,
+    basis, upd, plane_sem, out_sem, load_sem, route_send, route_recv, far_send, far_recv, z_send, z_recv,
+    one_send, one_recv, two_send, two_recv, core_send, core_recv, part_send, part_recv,
     ring_send, ring_recv, proj_send, proj_recv,
 ):
     me, z = lax.axis_index("expert"), lax.axis_index("dp")
@@ -319,13 +320,14 @@
     core, chip = lax.rem(me, 2), me // 2
     spot = (lax.rem(chip, wide), chip // wide)
     tokens, cols = rep.shape[2:]
-    half = tokens // 2
     experts, slots, units = hid.shape
     rank = 2 * fact.shape[1]
     cap = slots // n_expert
     top = routes.shape[2] // 2
-    group = mixed.shape[0]
-    span = n_expert // group
+    mate = z + 1 - 2 * lax.rem(z, 2)
+    cross = n_dp - 1 - z
+    replica = [z, cross, mate, lax.rem(z + 2, n_dp)]
+    order = [0, 2, 1, 3]
 
     def shifted(dim, by):
         return lax.rem(spot[dim] + by + sides[dim], sides[dim])
@@ -344,8 +346,8 @@
     def beside(i):
         return {"expert": lax.rem(me + i, n_expert)}
 
-    def along(k):
-        return {"dp": lax.rem(z + k, n_dp)}
+    def quarter(ref, at):
+        return ref.at[:, pl.ds(pl.multiple_of(at * cols, 128), cols)]
 
     loads = []
 
@@ -354,20 +356,25 @@
         copy.start()
         loads.append(copy)
 
-    for k in range(n_dp):
-        load(grads_ref.at[:, pl.ds(k * cols, cols)], rep.at[k, me])
-    for k in range(n_dp):
-        load(q_ref.at[:, pl.ds(k * cols, cols)], qv.at[k])
+    for m in (1, 3, 2):
+        load(quarter(grads_ref, replica[m]), own.at[m - 1])
+    load(quarter(q_ref, z), qall.at[me])
+    load(quarter(grads_ref, z), rep.at[0, me])
     for j in range(experts):
         load(hidden_ref.at[j], hid.at[j])
 
     barrier = pltpu.get_barrier_semaphore()
-    greeted = [along(k) for k in range(1, n_dp)] + [beside(i) for i in range(1, n_expert)]
+    greeted = [{"dp": replica[m]} for m in range(1, n_dp)]
+    greeted += [beside(i) for i in range(1, n_expert)]
     for peer in greeted:
         pl.semaphore_signal(barrier, inc=1, device_id=peer, device_id_type=MESH)
     routes[0, me] = jnp.concatenate([ids_ref[...].astype(F32), probs_ref[...]], axis=0)
     own_route = routes.at[0, me]
     pl.semaphore_wait(barrier, len(greeted))
+    for m in range(1, n_dp):
+        pl.semaphore_signal(
+            plane_sem, inc=1, device_id={"dp": replica[m]}, device_id_type=MESH
+        )
 
     sent = []
 
@@ -381,18 +388,22 @@
         return copy
 
     told, told_far, arrive_z = {}, {}, {}
-    for i in range(1, n_expert):
-        told[0, i] = push(
-            own_route, own_route, route_send.at[0, i], route_recv.at[0, i], beside(i)
-        )
-    for k in range(1, n_dp):
-        told_far[k] = push(own_route, routes.at[k, me], far_send.at[k], far_recv.at[k], along(k))
+    for m in (1, 3, 2):
+        told_far[m] = push(
+            own_route, routes.at[m, me], far_send.at[m], far_recv.at[m], {"dp": replica[m]}
+        )
+    for at, m in enumerate((1, 3, 2)):
+        loads[at].wait()
+        arrive_z[m] = push(
+            own.at[m - 1], rep.at[m, me], z_send.at[m], z_recv.at[m], {"dp": replica[m]}
+        )
 
     arrive_one, arrive_two, arrive_core = {}, {}, {}
 
     def rows(b, k, h):
-        own = rep.at[k, b] if k < n_dp else bulk.at[k - n_dp, b]
-        return own.at[pl.ds(h * half, half)]
+        whole = rep.at[k, b] if k < n_dp else qall.at[b]
+        half = whole.shape[0] // 2
+        return whole.at[pl.ds(h * half, half)]
 
     def swap(k, h, first, second):
         part = rows(source(h, first, second, core), k, h)
@@ -426,9 +437,9 @@
                 arrive_one[h, k, by - 1].wait_recv()
                 onward(k, h, by)
 
-    def second(k, low=0, high=None):
+    def second(k):
         for h in range(2):
-            for first in range(low, sides[h] if high is None else high):
+            for first in range(sides[h]):
                 for by in range(1, sides[1 - h]):
                     arrive_two[h, k, first, by - 1].wait_recv()
                     swap(k, h, first, by)
@@ -438,50 +449,30 @@
             if at[1] == k:
                 copy.wait_recv()
 
-    def gain(k, p):
-        piece = rep[k, pl.ds(p * span, span)].reshape(span * tokens, cols)
-        value = lax.dot_general(
-            qv[k], piece, (((1,), (1,)), ((), ())), preferred_element_type=F32
-        )
-        mixed[p] = value if k == 0 else mixed[p] + value
-
-    def accumulate(k):
-        loads[n_dp + k].wait()
-        landed(k)
-        for p in range(group):
-            gain(k, p)
-
-    def finish(k, far):
-        for x in range(sides[0]):
-            for y in range(sides[1]):
-                if (x > 0 and y > 0) == far:
-                    arrive_core[0, k, x, y].wait_recv()
-                    arrive_core[1, k, y, x].wait_recv()
-                    gain(k, source(0, x, y, 0) // 2)
-
-    def place_tokens(k):
-        for i in range(1, n_expert):
-            told[k, i].wait_recv()
-        ours = lax.broadcasted_iota(jnp.int32, (experts, tokens), 0) + me * experts
+    def matched(table, first, count):
+        ours = lax.broadcasted_iota(jnp.int32, (count, tokens), 0) + first
         ours = ours.astype(F32)
-        gates, hits = [], []
-        for b in range(n_expert):
-            table = routes[k, b]
-            value = jnp.zeros((experts, tokens), F32)
-            hit = jnp.zeros((experts, tokens), F32)
-            for t in range(top):
-                same = table[t : t + 1, :] == ours
-                value = jnp.where(same, table[top + t : top + t + 1, :], value)
-                hit = jnp.where(same, 1.0, hit)
-            gates.append(value)
-            hits.append(hit)
-        gate[k] = jnp.concatenate(gates, axis=1)
-        hits = jnp.concatenate(hits, axis=0)
+        value = jnp.zeros((count, tokens), F32)
+        hit = jnp.zeros((count, tokens), F32)
+        for t in range(top):
+            same = table[t : t + 1, :] == ours
+            value = jnp.where(same, table[top + t : top + t + 1, :], value)
+            hit = jnp.where(same, 1.0, hit)
+        return value, hit
+
+    def positions(hits):
         before = lax.broadcasted_iota(jnp.int32, (tokens, tokens), 0)
         after = lax.broadcasted_iota(jnp.int32, (tokens, tokens), 1)
         earlier = jnp.where(before < after, 1.0, 0.0).astype(BF16)
         count = jnp.dot(hits.astype(BF16), earlier, preferred_element_type=F32)
-        count = jnp.where(hits > 0.5, count, -float(slots))
+        return jnp.where(hits > 0.5, count, -float(slots))
+
+    def place_tokens(k):
+        for i in range(1, n_expert):
+            told[k, i].wait_recv()
+        found = [matched(routes[k, b], me * experts, experts) for b in range(n_expert)]
+        gate[k] = jnp.concatenate([value for value, _ in found], axis=1)
+        count = positions(jnp.concatenate([hit for _, hit in found], axis=0))
         keys = [
             count[b * experts : (b + 1) * experts] + float(b * cap) for b in range(n_expert)
         ]
@@ -490,46 +481,92 @@
         for j in range(experts):
             pick[k, j] = jnp.where(level == key[j : j + 1, :], 1.0, 0.0).astype(BF16)
 
-    for k in range(n_dp):
-        loads[k].wait()
-    for k in range(1, n_dp):
-        to = lax.rem(z + k, n_dp)
-        arrive_z[k] = push(
-            rep.at[to, me], bulk.at[k - 1, me], z_send.at[k], z_recv.at[k], along(k)
-        )
-    for k in range(n_dp + 2):
-        if k < n_dp:
-            begin(k)
-        if 0 <= k - 1 < n_dp:
-            forward(k - 1)
-        if k == 0:
-            place_tokens(0)
-        if k == n_dp:
-            for r in range(1, n_dp):
-                told_far[r].wait_recv()
-                for i in range(1, n_expert):
-                    told[r, i] = push(
-                        routes.at[r, me], routes.at[r, me],
-                        route_send.at[r, i], route_recv.at[r, i], beside(i),
-                    )
-            for r in range(1, n_dp):
-                arrive_z[r].wait_recv()
-                begin(n_dp + r - 1)
-        if 0 <= k - 3 < n_dp - 1:
-            accumulate(k - 3)
-        if 0 <= k - 2 < n_dp - 1:
-            second(k - 2)
-        if k == n_dp + 1:
-            second(n_dp - 1, 0, 1)
-    loads[2 * n_dp - 1].wait()
-    finish(n_dp - 1, False)
-    second(n_dp - 1, 1)
-    finish(n_dp - 1, True)
-    for copy in loads[2 * n_dp :]:
+    def place_near(m):
+        value, hit = matched(routes[m, me], 0, n_expert * experts)
+        near_gate[m] = value
+        key = positions(hit).astype(jnp.int32)
+        level = lax.broadcasted_iota(jnp.int32, (cap, tokens), 0)
+        for b in range(n_expert):
+            rows_of = [
+                jnp.where(level == key[b * experts + j : b * experts + j + 1, :], 1.0, 0.0)
+                for j in range(experts)
+            ]
+            near_pick[m, b] = jnp.concatenate(rows_of, axis=0).astype(BF16)
+
+    def folded(value, count, size):
+        line = lax.broadcasted_iota(jnp.int32, (rank, value.shape[1]), 1)
+        out = jnp.zeros((rank, value.shape[1]), F32)
+        for j in range(count):
+            mine = jnp.logical_and(line >= j * size, line < (j + 1) * size)
+            out = jnp.where(mine, value[j * rank : (j + 1) * rank], out)
+        return out
+
+    arrive_part = {}
+
+    def contract(ms):
+        for i in range(n_expert):
+            b = lax.rem(me + i, n_expert)
+            near = jnp.concatenate([rep[m, me] for m in ms], axis=0)
+            value = lax.dot_general(
+                qall[b], near, (((1,), (1,)), ((), ())), preferred_element_type=F32
+            )
+            for at, m in enumerate(ms):
+                scale = near_gate[m, pl.ds(pl.multiple_of(b * experts, experts), experts)]
+                one = value[:, at * tokens : (at + 1) * tokens]
+                one = one.reshape(experts, rank, tokens) * scale[:, None, :]
+                weighed[at, i] = one.reshape(experts * rank, tokens).astype(BF16)
+        for at, m in enumerate(ms):
+            for i in range(n_expert):
+                b = lax.rem(me + i, n_expert)
+                value = lax.dot_general(
+                    weighed[at, i], near_pick[m, b], (((1,), (1,)), ((), ())),
+                    preferred_element_type=F32,
+                )
+                message[m, i] = folded(value, experts, cap).astype(BF16)
+        for m in ms:
+            for i in range(n_expert):
+                if m == 0 and i == 0:
+                    parts[0, me] = message[0, 0]
+                    continue
+                arrive_part[m, i] = push(
+                    message.at[m, i], parts.at[m, me], part_send.at[m, i], part_recv.at[m, i],
+                    {"expert": lax.rem(me + i, n_expert), "dp": replica[m]},
+                )
+
+    loads[3].wait()
+    begin(n_dp)
+    across = lax.broadcasted_iota(jnp.int32, (slots, slots), 0)
+    along = lax.broadcasted_iota(jnp.int32, (slots, slots), 1)
+    along = along - cap * (along // cap)
+    for j in range(experts):
+        spots[j] = jnp.where(across == along + j * cap, 1.0, 0.0).astype(BF16)
+    for copy in loads[4:]:
         copy.wait()
-
-    mate = z + 1 - 2 * lax.rem(z, 2)
-    cross = n_dp - 1 - z
+    place_near(0)
+    forward(n_dp)
+    begin(0)
+    for m in range(1, n_dp):
+        told_far[m].wait_recv()
+        place_near(m)
+    second(n_dp)
+    pl.semaphore_wait(plane_sem, n_dp - 1)
+    arrive_z[2].wait_recv()
+    landed(n_dp)
+    contract((0, 2))
+    arrive_z[1].wait_recv()
+    contract((1,))
+    arrive_z[3].wait_recv()
+    contract((3,))
+    forward(0)
+    for m in order:
+        for i in range(1, n_expert):
+            told[m, i] = push(
+                routes.at[m, me], routes.at[m, me],
+                route_send.at[m, i], route_recv.at[m, i], beside(i),
+            )
+    for m in order[1:]:
+        begin(m)
+
     inner = jnp.logical_or(z == 1, z == 2)
 
     def hop(kind, j, src, dst, to):
@@ -548,12 +585,18 @@
     def down(j):
         return hop(2, j, tot, tot, mate)
 
+    for copy in arrive_part.values():
+        copy.wait_recv()
+    filled = []
+    for b in range(n_expert):
+        value = parts[0, b].astype(F32)
+        for m in range(1, n_dp):
+            value = value + parts[m, b].astype(F32)
+        filled.append(value.astype(BF16))
+    filled = jnp.concatenate(filled, axis=0)
     for j in range(experts):
-        value = jnp.concatenate([mixed[p, j * rank : (j + 1) * rank] for p in range(group)], axis=1)
-        value = (value * gate[0, j : j + 1, :]).astype(BF16)
-        value = lax.dot_general(
-            value, pick[0, j], (((1,), (1,)), ((), ())), preferred_element_type=F32
-        ).astype(BF16)
+        value = jnp.dot(filled, spots[j], preferred_element_type=F32)
+        value = folded(value, n_expert, cap).astype(BF16)
         value = jnp.dot(value, hid[j], preferred_element_type=F32).astype(BF16)
         fact[2 * j : 2 * j + 2] = value.reshape(2, rank // 2, units)
 
@@ -564,7 +607,6 @@
 
     ahead = 3
     pieces = 2 * experts
-    others = list(range(1, n_dp))
     for step in range(pieces + ahead):
         if step < pieces:
 
@@ -583,10 +625,14 @@
                 tot[j] = (fact[j].astype(F32) + got_cross[j].astype(F32)).astype(BF16)
                 down(j).start()
 
-        if step % 2 == 1 and step // 2 < len(others):
-            place_tokens(others[step // 2])
-    for r in range(1, n_dp):
-        forward(n_dp + r - 1)
+        if step in (1, 3, 5, 7):
+            place_tokens(order[step // 2])
+        if step == 9:
+            forward(2)
+        if step == 13:
+            forward(1)
+        if step == 17:
+            forward(3)
 
     shape = (rank, 2 * rank)
     eye = lax.broadcasted_iota(jnp.int32, shape, 1) == lax.broadcasted_iota(jnp.int32, shape, 0) + rank
@@ -638,10 +684,10 @@
             g = j // batch
             put(basis.at[pl.ds(g * batch, batch)], basis_ref.at[pl.ds(g * batch, batch)])
             part = pl.ds(g * batch // 2, batch // 2)
-            for k in range(1, n_dp):
+            for k in (3, 1, 2):
                 arrive_proj[k, g] = push(
                     proj.at[0, part], proj.at[k, part],
-                    proj_send.at[k, g], proj_recv.at[k, g], along(k),
+                    proj_send.at[k, g], proj_recv.at[k, g], {"dp": replica[k]},
                 )
 
     def update(k):
@@ -654,24 +700,22 @@
                 preferred_element_type=F32,
             )
             spr[j * rank : (j + 1) * rank] = (value * gate[k, j : j + 1, :]).astype(BF16)
-        if k:
-            landed(n_dp + k - 1)
-        own = bulk.at[k - 1] if k else rep.at[z]
-
+        landed(k)
         width = 256 if cols % 256 == 0 else 128
         for c in range(cols // width):
             at = slice(c * width, (c + 1) * width)
-            right = own[:, :, at].reshape(n_expert * tokens, width)
+            right = rep[k, :, :, at].reshape(n_expert * tokens, width)
             value = jnp.dot(spr[...], right, preferred_element_type=F32)
             upd[:, at] = upd[:, at] + value if k else value
-            if k == n_dp - 1:
+            if k == order[-1]:
                 put(upd.at[:, at], upd_ref.at[:, at])
 
-    update(0)
-    for r in range(1, n_dp):
-        second(n_dp + r - 1)
-    for r in range(1, n_dp):
-        update(r)
+    second(order[0])
+    second(order[1])
+    for at, m in enumerate(order):
+        update(m)
+        if at + 2 < n_dp:
+            second(order[at + 2])
     for j in range(pieces):
 
         @pl.when(inner)
@@ -691,19 +735,25 @@
 
 def fused_buffers(n_expert, n_dp, tokens, width, experts, slots, units, rank, top):
     cols = width // n_dp
+    halves = ((2 * experts, rank // 2, units), BF16)
     return [
         ((n_dp, n_expert, tokens, cols), BF16),
-        ((n_dp - 1, n_expert, tokens, cols), BF16),
+        ((n_dp - 1, tokens, cols), BF16),
         ((experts, slots, units), BF16),
-        ((n_dp, experts * rank, cols), BF16),
+        ((n_expert, experts * rank, cols), BF16),
         ((n_dp, n_expert, 2 * top, tokens), F32),
         ((n_dp, experts, n_expert * tokens), F32),
         ((n_dp, experts, slots, n_expert * tokens), BF16),
-        ((n_expert // 2, experts * rank, 2 * tokens), F32),
-        ((2 * experts, rank // 2, units), BF16),
-        ((2 * experts, rank // 2, units), BF16),
-        ((2 * experts, rank // 2, units), BF16),
-        ((2 * experts, rank // 2, units), BF16),
+        ((n_dp, n_expert * experts, tokens), F32),
+        ((n_dp, n_expert, slots, tokens), BF16),
+        ((2, n_expert, experts * rank, tokens), BF16),
+        ((n_dp, n_expert, rank, slots), BF16),
+        ((n_dp, n_expert, rank, slots), BF16),
+        ((experts, slots, slots), BF16),
+        halves,
+        halves,
+        halves,
+        halves,
         ((experts, rank, 2 * rank), F32),
         ((n_dp, experts // 2, rank, 2 * slots), BF16),
         ((experts * rank, n_expert * tokens), BF16),
@@ -719,7 +769,7 @@
     cols = q.shape[1] // n_dp
     chips = n_expert // 2
     long = max(math.isqrt(chips), chips // math.isqrt(chips))
-    tags = 2 * n_dp - 1
+    tags = n_dp + 1
     dma = pltpu.SemaphoreType.DMA
     vmem = pl.BlockSpec(memory_space=pltpu.VMEM)
     anywhere = pl.BlockSpec(memory_space=pl.ANY)
@@ -732,12 +782,13 @@
         in_specs=[anywhere, vmem, vmem, anywhere, anywhere],
         out_specs=(anywhere, anywhere),
         scratch_shapes=[pltpu.VMEM(*b) for b in buffers] + [
-            dma((2 + cols // 128,)), dma((2 * n_dp + experts,)),
+            pltpu.SemaphoreType.REGULAR, dma((2 + cols // 128,)), dma((n_dp + 1 + experts,)),
             dma((n_dp, n_expert)), dma((n_dp, n_expert)), dma((n_dp,)), dma((n_dp,)),
             dma((n_dp,)), dma((n_dp,)),
             dma((2, tags, long - 1)), dma((2, tags, long - 1)),
             dma((2, tags, long, long - 1)), dma((2, tags, long, long - 1)),
             dma((2, tags, long, long)), dma((2, tags, long, long)),
+            dma((n_dp, n_expert)), dma((n_dp, n_expert)),
             dma((3, 2 * experts)), dma((3, 2 * experts)), dma((n_dp, 2)), dma((n_dp, 2)),
         ],
         compiler_params=pltpu.CompilerParams(

time: 131 us -> 120 us (0.916)
  Pallas kernels: 125 us -> 115 us
    pallas_call x1, Pallas kernels: 125 us -> 115 us  [fused(): pl.pallas_call(functools.partial(fused_kernel, n_expert, n_dp), out_shape...]
where the time goes in v4:
time: 120 us
  Pallas kernels  115 us (96%)
  local copies, waits for them, and re-layouts  4.5 us (4%)
    pallas_call x1, Pallas kernels, fused(): pl.pallas_call(functools.partial(fused_kernel, n_expert, n_dp), out_shape...  115 us
    unnamed x4, local copies, waits for them, and re-layouts  4.5 us

profile of v4, /device:TPU:0, one launch (start us, length us, event | category | flops | bytes accessed | tf_op | source)
XLA Modules:
  0.0 119.8 jit_solution(1453059224115741323)
XLA Ops:
  0.6 114.7 %fused.1 = (f32[8,32,2048]{2,1,0:T(8,128)}, f32[256,1792]{1,0:T(8,128)}) custom-call(bf16[128,7168]{1,0:T(8,128)(2,1)} %bitcast.12, s32[8,128]{1,0:T(8,128)} %bitcast.14, f32[8,128]{1,0:T(8,128)} %bitcast.15, bf16[8,192,2048]{2,1,0:T(8,128)(2,1)} %bitcast.10, bf16[256,7168]{1,0:T(8,128)(2,1)} %bitcast.11), custom_call_target="tpu_custom_call" | custom-call | tf_op jit(solution)/shard_map/fused/pallas_call | solution.py:776
  115.3 0.0 copy-start
  115.3 3.3 %copy.9 = f32[8,32,2048]{2,1,0:T(8,128)} copy(f32[8,32,2048]{2,1,0:T(8,128)} %get-tuple-element.8) | data formatting | bytes 4194304
  118.6 0.0 copy-done
  118.6 1.2 %copy.10 = f32[8,32,1792]{2,1,0:T(8,128)} copy(f32[8,32,1792]{2,1,0:T(8,128)S(1)} %bitcast.13) | data formatting | bytes 3670016
Async XLA Ops:
  115.3 3.3 %copy-start = (f32[256,1792]{1,0:T(8,128)S(1)}, f32[256,1792]{1,0:T(8,128)}, u32[]{:S(2)}) copy-start(f32[256,1792]{1,0:T(8,128)} %get-tuple-element.5) | copy-start | bytes 5505028

commit v5 on v4

--- a/solution.py
+++ b/solution.py
@@ -310,7 +310,7 @@
     rep, own, hid, qall, routes, gate, pick, near_gate, near_pick, weighed, message, parts, spots,
     fact, got_up, got_cross, tot, gram, proj, spr,
     basis, upd, plane_sem, out_sem, load_sem, route_send, route_recv, far_send, far_recv, z_send, z_recv,
-    one_send, one_recv, two_send, two_recv, core_send, core_recv, part_send, part_recv,
+    hop_send, one_recv, two_recv, core_recv, part_send, part_recv,
     ring_send, ring_recv, proj_send, proj_recv,
 ):
     me, z = lax.axis_index("expert"), lax.axis_index("dp")
@@ -351,8 +351,8 @@
 
     loads = []
 
-    def load(src, dst):
-        copy = pltpu.make_async_copy(src, dst, load_sem.at[len(loads)])
+    def load(src, dst, at=None):
+        copy = pltpu.make_async_copy(src, dst, load_sem.at[len(loads) if at is None else at])
         copy.start()
         loads.append(copy)
 
@@ -361,7 +361,7 @@
     load(quarter(q_ref, z), qall.at[me])
     load(quarter(grads_ref, z), rep.at[0, me])
     for j in range(experts):
-        load(hidden_ref.at[j], hid.at[j])
+        load(hidden_ref.at[j], hid.at[j], n_dp + 1)
 
     barrier = pltpu.get_barrier_semaphore()
     greeted = [{"dp": replica[m]} for m in range(1, n_dp)]
@@ -376,7 +376,11 @@
             plane_sem, inc=1, device_id={"dp": replica[m]}, device_id_type=MESH
         )
 
-    sent = []
+    def awaited(ref, sem):
+        return pltpu.make_async_remote_copy(
+            src_ref=ref, dst_ref=ref, send_sem=sem, recv_sem=sem,
+            device_id={"dp": mate}, device_id_type=MESH,
+        )
 
     def push(src, dst, send_sem, recv_sem, device):
         copy = pltpu.make_async_remote_copy(
@@ -384,21 +388,20 @@
             device_id=device, device_id_type=MESH,
         )
         copy.start()
-        sent.append(copy)
         return copy
 
-    told, told_far, arrive_z = {}, {}, {}
+    told_far, arrive_z = {}, {}
     for m in (1, 3, 2):
         told_far[m] = push(
-            own_route, routes.at[m, me], far_send.at[m], far_recv.at[m], {"dp": replica[m]}
+            own_route, routes.at[m, me], far_send, far_recv.at[m], {"dp": replica[m]}
         )
     for at, m in enumerate((1, 3, 2)):
         loads[at].wait()
         arrive_z[m] = push(
-            own.at[m - 1], rep.at[m, me], z_send.at[m], z_recv.at[m], {"dp": replica[m]}
-        )
-
-    arrive_one, arrive_two, arrive_core = {}, {}, {}
+            own.at[m - 1], rep.at[m, me], z_send, z_recv.at[m], {"dp": replica[m]}
+        )
+
+    arrive_one, arrive_two = {}, {}
 
     def rows(b, k, h):
         whole = rep.at[k, b] if k < n_dp else qall.at[b]
@@ -407,16 +410,15 @@
 
     def swap(k, h, first, second):
         part = rows(source(h, first, second, core), k, h)
-        at = (h, k, first, second)
         partner = {"expert": block(spot[0], spot[1], 1 - core)}
-        arrive_core[at] = push(part, part, core_send.at[at], core_recv.at[at], partner)
+        push(part, part, hop_send.at[k], core_recv.at[k], partner)
 
     def onward(k, h, first):
         part = rows(source(h, first, 0, core), k, h)
         for by in range(1, sides[1 - h]):
             at = (h, k, first, by - 1)
             arrive_two[at] = push(
-                part, part, two_send.at[at], two_recv.at[at], {"expert": neighbour(1 - h, by)}
+                part, part, hop_send.at[k], two_recv.at[at], {"expert": neighbour(1 - h, by)}
             )
         swap(k, h, first, 0)
 
@@ -426,7 +428,7 @@
             for by in range(1, sides[h]):
                 at = (h, k, by - 1)
                 arrive_one[at] = push(
-                    part, part, one_send.at[at], one_recv.at[at], {"expert": neighbour(h, by)}
+                    part, part, hop_send.at[k], one_recv.at[at], {"expert": neighbour(h, by)}
                 )
         for h in range(2):
             onward(k, h, 0)
@@ -445,9 +447,8 @@
                     swap(k, h, first, by)
 
     def landed(k):
-        for at, copy in arrive_core.items():
-            if at[1] == k:
-                copy.wait_recv()
+        whole = rep.at[k] if k < n_dp else qall
+        awaited(whole.at[pl.ds(0, chips)], core_recv.at[k]).wait_recv()
 
     def matched(table, first, count):
         ours = lax.broadcasted_iota(jnp.int32, (count, tokens), 0) + first
@@ -468,8 +469,7 @@
         return jnp.where(hits > 0.5, count, -float(slots))
 
     def place_tokens(k):
-        for i in range(1, n_expert):
-            told[k, i].wait_recv()
+        awaited(routes.at[k, pl.ds(0, n_expert - 1)], route_recv.at[k]).wait_recv()
         found = [matched(routes[k, b], me * experts, experts) for b in range(n_expert)]
         gate[k] = jnp.concatenate([value for value, _ in found], axis=1)
         count = positions(jnp.concatenate([hit for _, hit in found], axis=0))
@@ -500,8 +500,6 @@
             mine = jnp.logical_and(line >= j * size, line < (j + 1) * size)
             out = jnp.where(mine, value[j * rank : (j + 1) * rank], out)
         return out
-
-    arrive_part = {}
 
     def contract(ms):
         for i in range(n_expert):
@@ -528,8 +526,9 @@
                 if m == 0 and i == 0:
                     parts[0, me] = message[0, 0]
                     continue
-                arrive_part[m, i] = push(
-                    message.at[m, i], parts.at[m, me], part_send.at[m, i], part_recv.at[m, i],
+                push(
+                    message.at[m, i], parts.at[m, me],
+                    part_send.at[min(m, 1)], part_recv.at[min(m, 1)],
                     {"expert": lax.rem(me + i, n_expert), "dp": replica[m]},
                 )
 
@@ -540,8 +539,8 @@
     along = along - cap * (along // cap)
     for j in range(experts):
         spots[j] = jnp.where(across == along + j * cap, 1.0, 0.0).astype(BF16)
-    for copy in loads[4:]:
-        copy.wait()
+    loads[4].wait()
+    pltpu.make_async_copy(hidden_ref, hid, load_sem.at[n_dp + 1]).wait()
     place_near(0)
     forward(n_dp)
     begin(0)
@@ -555,15 +554,12 @@
     contract((0, 2))
     arrive_z[1].wait_recv()
     contract((1,))
-    arrive_z[3].wait_recv()
-    contract((3,))
     forward(0)
     for m in order:
         for i in range(1, n_expert):
-            told[m, i] = push(
-                routes.at[m, me], routes.at[m, me],
-                route_send.at[m, i], route_recv.at[m, i], beside(i),
-            )
+            push(routes.at[m, me], routes.at[m, me], route_send, route_recv.at[m], beside(i))
+    arrive_z[3].wait_recv()
+    contract((3,))
     for m in order[1:]:
         begin(m)
 
@@ -572,7 +568,7 @@
     def hop(kind, j, src, dst, to):
         return pltpu.make_async_remote_copy(
             src_ref=src.at[j], dst_ref=dst.at[j],
-            send_sem=ring_send.at[kind, j], recv_sem=ring_recv.at[kind, j],
+            send_sem=ring_send.at[kind], recv_sem=ring_recv.at[kind, j],
             device_id={"dp": to}, device_id_type=MESH,
         )
 
@@ -585,8 +581,9 @@
     def down(j):
         return hop(2, j, tot, tot, mate)
 
-    for copy in arrive_part.values():
-        copy.wait_recv()
+    near_parts, far_parts = pl.ds(0, n_expert - 1), pl.ds(1, n_dp - 1)
+    awaited(parts.at[0, near_parts], part_recv.at[0]).wait_recv()
+    awaited(parts.at[far_parts], part_recv.at[1]).wait_recv()
     filled = []
     for b in range(n_expert):
         value = parts[0, b].astype(F32)
@@ -661,12 +658,9 @@
         gram[:, k, :] = table[k].T
 
     batch = experts // 2
-    arrive_proj, stored = {}, []
-
-    def put(src, dst):
-        copy = pltpu.make_async_copy(src, dst, out_sem.at[len(stored)])
-        copy.start()
-        stored.append(copy)
+
+    def put(src, dst, at):
+        pltpu.make_async_copy(src, dst, out_sem.at[at]).start()
 
     for j in range(experts):
         inverse = gram[j][:, rank:]
@@ -682,18 +676,17 @@
         ).astype(BF16)
         if (j + 1) % batch == 0:
             g = j // batch
-            put(basis.at[pl.ds(g * batch, batch)], basis_ref.at[pl.ds(g * batch, batch)])
+            put(basis.at[pl.ds(g * batch, batch)], basis_ref.at[pl.ds(g * batch, batch)], 0)
             part = pl.ds(g * batch // 2, batch // 2)
             for k in (3, 1, 2):
-                arrive_proj[k, g] = push(
+                push(
                     proj.at[0, part], proj.at[k, part],
-                    proj_send.at[k, g], proj_recv.at[k, g], {"dp": replica[k]},
+                    proj_send, proj_recv.at[k], {"dp": replica[k]},
                 )
 
     def update(k):
         if k:
-            for g in range(2):
-                arrive_proj[k, g].wait_recv()
+            awaited(proj.at[k], proj_recv.at[k]).wait_recv()
         for j in range(experts):
             value = jnp.dot(
                 proj[k, j // 2, :, (j % 2) * slots : (j % 2 + 1) * slots], pick[k, j],
@@ -708,7 +701,7 @@
             value = jnp.dot(spr[...], right, preferred_element_type=F32)
             upd[:, at] = upd[:, at] + value if k else value
             if k == order[-1]:
-                put(upd.at[:, at], upd_ref.at[:, at])
+                put(upd.at[:, at], upd_ref.at[:, at], 1)
 
     second(order[0])
     second(order[1])
@@ -716,21 +709,27 @@
         update(m)
         if at + 2 < n_dp:
             second(order[at + 2])
-    for j in range(pieces):
-
-        @pl.when(inner)
-        def _():
-            over(j).wait_send()
-            down(j).wait_send()
-
-        @pl.when(jnp.logical_not(inner))
-        def _():
-            up(j).wait_send()
-
-    for copy in sent:
-        copy.wait_send()
-    for copy in stored:
-        copy.wait()
+
+    @pl.when(inner)
+    def _():
+        awaited(fact, ring_send.at[1]).wait_send()
+        awaited(tot, ring_send.at[2]).wait_send()
+
+    @pl.when(jnp.logical_not(inner))
+    def _():
+        awaited(fact, ring_send.at[0]).wait_send()
+
+    for k in range(n_dp):
+        awaited(rep.at[k, near_parts], hop_send.at[k]).wait_send()
+    awaited(qall.at[near_parts], hop_send.at[n_dp]).wait_send()
+    awaited(routes.at[:, near_parts], route_send).wait_send()
+    awaited(routes.at[0, pl.ds(0, n_dp - 1)], far_send).wait_send()
+    awaited(own, z_send).wait_send()
+    awaited(message.at[0, near_parts], part_send.at[0]).wait_send()
+    awaited(message.at[far_parts], part_send.at[1]).wait_send()
+    awaited(proj.at[far_parts], proj_send).wait_send()
+    pltpu.make_async_copy(basis, basis_ref, out_sem.at[0]).wait()
+    pltpu.make_async_copy(upd, upd_ref, out_sem.at[1]).wait()
 
 
 def fused_buffers(n_expert, n_dp, tokens, width, experts, slots, units, rank, top):
@@ -782,14 +781,10 @@
         in_specs=[anywhere, vmem, vmem, anywhere, anywhere],
         out_specs=(anywhere, anywhere),
         scratch_shapes=[pltpu.VMEM(*b) for b in buffers] + [
-            pltpu.SemaphoreType.REGULAR, dma((2 + cols // 128,)), dma((n_dp + 1 + experts,)),
-            dma((n_dp, n_expert)), dma((n_dp, n_expert)), dma((n_dp,)), dma((n_dp,)),
-            dma((n_dp,)), dma((n_dp,)),
-            dma((2, tags, long - 1)), dma((2, tags, long - 1)),
-            dma((2, tags, long, long - 1)), dma((2, tags, long, long - 1)),
-            dma((2, tags, long, long)), dma((2, tags, long, long)),
-            dma((n_dp, n_expert)), dma((n_dp, n_expert)),
-            dma((3, 2 * experts)), dma((3, 2 * experts)), dma((n_dp, 2)), dma((n_dp, 2)),
+            pltpu.SemaphoreType.REGULAR, dma((2,)), dma((n_dp + 2,)),
+            dma(()), dma((n_dp,)), dma(()), dma((n_dp,)), dma(()), dma((n_dp,)),
+            dma((tags,)), dma((2, tags, long - 1)), dma((2, tags, long, long - 1)), dma((tags,)),
+            dma((2,)), dma((2,)), dma((3,)), dma((3, 2 * experts)), dma(()), dma((n_dp,)),
         ],
         compiler_params=pltpu.CompilerParams(
             collective_id=2, has_side_effects=True, vmem_limit_bytes=67043328

time: 120 us -> 116 us (0.967)
  Pallas kernels: 115 us -> 110 us
    pallas_call x1, Pallas kernels: 115 us -> 110 us  [fused(): pl.pallas_call(functools.partial(fused_kernel, n_expert, n_dp), out_shape...]
where the time goes in v5:
time: 116 us
  Pallas kernels  110 us (95%)
  local copies, waits for them, and re-layouts  4.5 us (4%)
    pallas_call x1, Pallas kernels, fused(): pl.pallas_call(functools.partial(fused_kernel, n_expert, n_dp), out_shape...  110 us
    unnamed x4, local copies, waits for them, and re-layouts  4.5 us

profile of v5, /device:TPU:0, one launch (start us, length us, event | category | flops | bytes accessed | tf_op | source)
XLA Modules:
  0.0 115.5 jit_solution(7386541409053394339)
XLA Ops:
  0.6 110.4 %fused.1 = (f32[8,32,2048]{2,1,0:T(8,128)}, f32[256,1792]{1,0:T(8,128)}) custom-call(bf16[128,7168]{1,0:T(8,128)(2,1)} %bitcast.12, s32[8,128]{1,0:T(8,128)} %bitcast.14, f32[8,128]{1,0:T(8,128)} %bitcast.15, bf16[8,192,2048]{2,1,0:T(8,128)(2,1)} %bitcast.10, bf16[256,7168]{1,0:T(8,128)(2,1)} %bitcast.11), custom_call_target="tpu_custom_call" | custom-call | tf_op jit(solution)/shard_map/fused/pallas_call | solution.py:775
  111.0 0.0 copy-start
  111.0 3.3 %copy.9 = f32[8,32,2048]{2,1,0:T(8,128)} copy(f32[8,32,2048]{2,1,0:T(8,128)} %get-tuple-element.8) | data formatting | bytes 4194304
  114.3 0.0 copy-done
  114.3 1.2 %copy.10 = f32[8,32,1792]{2,1,0:T(8,128)} copy(f32[8,32,1792]{2,1,0:T(8,128)S(1)} %bitcast.13) | data formatting | bytes 3670016
Async XLA Ops:
  111.0 3.3 %copy-start = (f32[256,1792]{1,0:T(8,128)S(1)}, f32[256,1792]{1,0:T(8,128)}, u32[]{:S(2)}) copy-start(f32[256,1792]{1,0:T(8,128)} %get-tuple-element.5) | copy-start | bytes 5505028

commit v6 on v5

--- a/solution.py
+++ b/solution.py
@@ -501,6 +501,23 @@
             out = jnp.where(mine, value[j * rank : (j + 1) * rank], out)
         return out
 
+    packs = message.shape[3] != slots
+    edge = slots // 128 * 128
+
+    def packed(value):
+        if not packs:
+            return value
+        tail = value[:, edge:]
+        tail = jnp.concatenate([tail[: rank // 2], tail[rank // 2 :]], axis=1)
+        return jnp.concatenate([value[:, :edge], tail], axis=0)
+
+    def unpacked(value):
+        if not packs:
+            return value
+        tail = value[rank:]
+        tail = jnp.concatenate([tail[:, : edge // 2], tail[:, edge // 2 :]], axis=0)
+        return jnp.concatenate([value[:rank], tail], axis=1)
+
     def contract(ms):
         for i in range(n_expert):
             b = lax.rem(me + i, n_expert)
@@ -520,7 +537,7 @@
                     weighed[at, i], near_pick[m, b], (((1,), (1,)), ((), ())),
                     preferred_element_type=F32,
                 )
-                message[m, i] = folded(value, experts, cap).astype(BF16)
+                message[m, i] = packed(folded(value, experts, cap)).astype(BF16)
         for m in ms:
             for i in range(n_expert):
                 if m == 0 and i == 0:
@@ -589,7 +606,7 @@
         value = parts[0, b].astype(F32)
         for m in range(1, n_dp):
             value = value + parts[m, b].astype(F32)
-        filled.append(value.astype(BF16))
+        filled.append(unpacked(value).astype(BF16))
     filled = jnp.concatenate(filled, axis=0)
     for j in range(experts):
         value = jnp.dot(filled, spots[j], preferred_element_type=F32)
@@ -735,6 +752,7 @@
 def fused_buffers(n_expert, n_dp, tokens, width, experts, slots, units, rank, top):
     cols = width // n_dp
     halves = ((2 * experts, rank // 2, units), BF16)
+    flat = (rank * 3 // 2, 128) if 2 * slots == 3 * 128 and rank % 32 == 0 else (rank, slots)
     return [
         ((n_dp, n_expert, tokens, cols), BF16),
         ((n_dp - 1, tokens, cols), BF16),
@@ -746,8 +764,8 @@
         ((n_dp, n_expert * experts, tokens), F32),
         ((n_dp, n_expert, slots, tokens), BF16),
         ((2, n_expert, experts * rank, tokens), BF16),
-        ((n_dp, n_expert, rank, slots), BF16),
-        ((n_dp, n_expert, rank, slots), BF16),
+        ((n_dp, n_expert, *flat), BF16),
+        ((n_dp, n_expert, *flat), BF16),
         ((experts, slots, slots), BF16),
         halves,
         halves,

time: 116 us -> 114 us (0.983)
    pallas_call x1, Pallas kernels: 110 us -> 109 us  [fused(): pl.pallas_call(functools.partial(fused_kernel, n_expert, n_dp), out_shape...]
where the time goes in v6:
time: 114 us
  Pallas kernels  109 us (96%)
  local copies, waits for them, and re-layouts  4.5 us (4%)
    pallas_call x1, Pallas kernels, fused(): pl.pallas_call(functools.partial(fused_kernel, n_expert, n_dp), out_shape...  109 us
    unnamed x4, local copies, waits for them, and re-layouts  4.5 us

profile of v6, /device:TPU:0, one launch (start us, length us, event | category | flops | bytes accessed | tf_op | source)
XLA Modules:
  0.0 113.9 jit_solution(7305425609996690738)
XLA Ops:
  0.6 108.8 %fused.1 = (f32[8,32,2048]{2,1,0:T(8,128)}, f32[256,1792]{1,0:T(8,128)}) custom-call(bf16[128,7168]{1,0:T(8,128)(2,1)} %bitcast.12, s32[8,128]{1,0:T(8,128)} %bitcast.14, f32[8,128]{1,0:T(8,128)} %bitcast.15, bf16[8,192,2048]{2,1,0:T(8,128)(2,1)} %bitcast.10, bf16[256,7168]{1,0:T(8,128)(2,1)} %bitcast.11), custom_call_target="tpu_custom_call" | custom-call | tf_op jit(solution)/shard_map/fused/pallas_call | solution.py:793
  109.4 0.0 copy-start
  109.4 3.3 %copy.9 = f32[8,32,2048]{2,1,0:T(8,128)} copy(f32[8,32,2048]{2,1,0:T(8,128)} %get-tuple-element.8) | data formatting | bytes 4194304
  112.7 0.0 copy-done
  112.7 1.2 %copy.10 = f32[8,32,1792]{2,1,0:T(8,128)} copy(f32[8,32,1792]{2,1,0:T(8,128)S(1)} %bitcast.13) | data formatting | bytes 3670016
Async XLA Ops:
  109.4 3.3 %copy-start = (f32[256,1792]{1,0:T(8,128)S(1)}, f32[256,1792]{1,0:T(8,128)}, u32[]{:S(2)}) copy-start(f32[256,1792]{1,0:T(8,128)} %get-tuple-element.5) | copy-start | bytes 5505028
